TPU v7x, 256 devices: a 4x2x16 block of a 4x16x16 slice. The times are simulated.
256 devices in a mesh: groups: 2 (over y), mesh: 16 (over z), edge: 8 (over x, core).
Axes of the slice: x: 4, y: 2, z: 16, core: 2. Of those that a mesh axis runs over, the one named last changes fastest.
The devices are a block of a 4x16x16 slice.
Arguments:
- grid_input: bfloat16 [131072, 474], P(('groups', 'mesh', 'edge')), parts along dimension 0, may hold values from -6 to 6
- mesh_position: bfloat16 [3, 2048], P(None, ('mesh', 'edge')), may hold values from -1 to 1
- encoder_senders: int32 [262144], P(('mesh', 'edge')), may hold values from 0 to 65535, as said below
- encoder_receivers: int32 [262144], P(('mesh', 'edge')), may hold values from 0 to 2047, as said below
- encoder_features: bfloat16 [4, 262144], P(None, ('mesh', 'edge')), may hold values from -6 to 6
- encoder_counts: int32 [128], P(('mesh', 'edge')), may hold values from 1 to 16, as said below
- mesh_senders: int32 [32768], P(('mesh', 'edge')), may hold values from 0 to 2047, as said below
- mesh_receivers: int32 [32768], P(('mesh', 'edge')), may hold values from 0 to 2047, as said below
- mesh_features: bfloat16 [4, 32768], P(None, ('mesh', 'edge')), may hold values from -6 to 6
- cotangent: bfloat16 [4096, 512], P(('groups', 'mesh', 'edge')), parts along dimension 0, may hold values from -6 to 6
- grid_first: bfloat16 [474, 512], replicated, may hold values from -0.25 to 0.25
- grid_second: bfloat16 [512, 512], replicated, may hold values from -0.25 to 0.25
- encoder_inner: bfloat16 [512, 512], replicated, may hold values from -0.25 to 0.25
- encoder_geometry: bfloat16 [4, 512], replicated, may hold values from -3 to 3
- encoder_outer: bfloat16 [512, 512], replicated, may hold values from -0.25 to 0.25
- node_first: bfloat16 [512, 512], replicated, may hold values from -0.25 to 0.25
- node_position: bfloat16 [3, 512], replicated, may hold values from -3.5 to 3.5
- node_second: bfloat16 [512, 512], replicated, may hold values from -0.25 to 0.25
- edge_sender: bfloat16 [512, 512], replicated, may hold values from -0.25 to 0.25
- edge_receiver: bfloat16 [512, 512], replicated, may hold values from -0.25 to 0.25
- edge_geometry: bfloat16 [4, 512], replicated, may hold values from -3 to 3
- edge_outer: bfloat16 [512, 512], replicated, may hold values from -0.25 to 0.25
- update_message: bfloat16 [512, 512], replicated, may hold values from -0.25 to 0.25
- update_state: bfloat16 [512, 512], replicated, may hold values from -0.25 to 0.25
- update_outer: bfloat16 [512, 512], replicated, may hold values from -0.25 to 0.25
Outputs:
- mesh_output: bfloat16 [4096, 512], P(('groups', 'mesh', 'edge')), parts along dimension 0
- mesh_gradient: float32 [4096, 512], P(('groups', 'mesh', 'edge')), parts along dimension 0
There are 2 independent parts, one for each index of `groups`. A program takes and returns all parts, laid end to end along the dimension named above; an argument that names none is the same for every part. Nothing has to cross between parts.
Inputs may be any that keep to these rules, and one draw needn't show every extreme that they name: `encoder_senders`: an encoder edge slot of a device with mesh index b has its sender in band b: from b * 4096 to (b + 1) * 4096 - 1. `encoder_receivers`: an encoder edge slot of a device with mesh index b has its receiver among the mesh nodes b * 128 to (b + 1) * 128 - 1. `encoder_counts`: slots in blocks at or beyond a device's count carry no edge. For every mesh index, one device of the edge axis has all 16 blocks live. `mesh_receivers`: A multimesh edge of a device with mesh index b has its receiver among the mesh nodes b * 128 to (b + 1) * 128 - 1. `mesh_senders`: A multimesh edge of a device with mesh index b has its sender either among the mesh nodes b * 128 to (b + 1) * 128 - 1, or at a node n with n mod 16 below 4.
All inputs are finite; a program needn't handle non-finite values.
Results may differ from a plain program's by a relative error of at most 0.039.
Values may be sent and summed in bfloat16 or wider, within the bound.
A program may use at most 128 MiB of HBM per device.

v0:
```python
import jax
import jax.numpy as jnp
from jax import lax
from jax.sharding import Mesh
from jax.sharding import PartitionSpec as P

BLOCK = 128
EDGE = ("edge_0", "edge_1")
MESH_EDGE = ("mesh", "edge_0", "edge_1")
GROUPS_MESH_EDGE = ("groups", "mesh", "edge_0", "edge_1")


def in_order(blocks, dim):
    blocks = jnp.moveaxis(blocks, 0, dim)
    dims = blocks.shape
    return blocks.reshape(*dims[:dim], dims[dim] * dims[dim + 1], *dims[dim + 2 :])


def copy_for_each(value, axis):
    copies = jnp.broadcast_to(value, (lax.axis_size(axis), *value.shape))
    return lax.all_to_all(copies, axis, split_axis=0, concat_axis=0, tiled=True)


def collect(value, axis, dim):
    return in_order(copy_for_each(value, axis), dim)


def in_blocks(value, dim, size):
    before, after = (value.shape[:dim], value.shape[dim + 1 :])
    return jnp.moveaxis(value.reshape(*before, size, -1, *after), dim, 0)


def sent_and_summed(value, axis, dim):
    blocks = in_blocks(value, dim, lax.axis_size(axis))
    arrived = lax.all_to_all(blocks, axis, split_axis=0, concat_axis=0, tiled=True)
    return arrived.astype(jnp.float32).sum(axis=0)


def all_blocks(value, axes, turns):
    blocks = value[None]
    for k in turns:
        blocks = lax.all_gather(blocks, axes[k], axis=0, tiled=True)
    block = [lax.axis_size(axes[k]) for k in reversed(turns)]
    blocks = blocks.reshape(*block, *value.shape)
    turned = sorted(range(len(turns)), key=lambda place: turns[len(turns) - 1 - place])
    return blocks.transpose(*turned, *range(len(turns), blocks.ndim)).reshape(-1, *value.shape)


def whole_of(value, axes, turns, dim):
    return in_order(all_blocks(value, axes, turns), dim)


def own_block_2(blocks, axes, turns):
    dims = [lax.axis_size(a) for a in axes]
    blocks = blocks.reshape(*dims, *blocks.shape[1:])
    blocks = blocks.transpose(*turns, *range(len(axes), blocks.ndim))
    blocks = blocks.reshape(-1, *blocks.shape[len(axes) :])
    for k in turns:
        blocks = lax.psum_scatter(blocks, axes[k], scatter_dimension=0, tiled=True)
    return blocks[0]


def scatter_axes(value, axes, turns, dim):
    size = lax.axis_size(axes)
    return own_block_2(in_blocks(value, dim, size), axes, turns)


def product(left, right):
    return jnp.dot(left, right, preferred_element_type=jnp.float32)


def layer_norm(values):
    centred = values - jnp.mean(values, axis=-1, keepdims=True)
    variance = jnp.mean(centred * centred, axis=-1, keepdims=True)
    return centred * lax.rsqrt(variance + 1e-05)


def silu_grad(values):
    sigma = jax.nn.sigmoid(values)
    return sigma * (1.0 + values * (1.0 - sigma))


def embed_grid(grid_rows, grid_first, grid_second):
    grid_hidden = jax.nn.silu(product(grid_rows, grid_first)).astype(jnp.bfloat16)
    return layer_norm(product(grid_hidden, grid_second)).astype(jnp.bfloat16)


def add_rows(row_count, targets, values):
    selector = (targets[None, :] == jnp.arange(row_count, dtype=jnp.int32)[:, None]).astype(
        jnp.float32
    )
    return jnp.dot(
        selector, values, precision=lax.Precision.HIGHEST, preferred_element_type=jnp.float32
    )


def shards(
    grid_input,
    mesh_position,
    encoder_senders,
    encoder_receivers,
    encoder_features,
    encoder_counts,
    mesh_senders,
    mesh_receivers,
    mesh_features,
    cotangent,
    grid_first,
    grid_second,
    encoder_inner,
    encoder_geometry,
    encoder_outer,
    node_first,
    node_position,
    node_second,
    edge_sender,
    edge_receiver,
    edge_geometry,
    edge_outer,
    update_message,
    update_state,
    update_outer,
):
    band_number = lax.axis_index("mesh")
    edge_count = lax.axis_size(EDGE)
    band_rows = grid_input.shape[0] * edge_count
    mesh_rows = mesh_position.shape[1]
    shard_rows = mesh_rows * edge_count
    width = grid_second.shape[1]
    band_latent = collect(embed_grid(grid_input, grid_first, grid_second), EDGE, 0)
    local_senders = encoder_senders - band_number * band_rows
    local_receivers = encoder_receivers - band_number * shard_rows

    def add_block(partial_value, senders_table, receivers_table, features_table, position):
        sender_rows = lax.dynamic_slice_in_dim(senders_table, position, BLOCK, 0)
        receiver_rows = lax.dynamic_slice_in_dim(receivers_table, position, BLOCK, 0)
        feature_rows = lax.dynamic_slice_in_dim(features_table, position, BLOCK, 1)
        enc_pre = product(jnp.take(band_latent, sender_rows, axis=0), encoder_inner)
        enc_pre = enc_pre + product(feature_rows.T, encoder_geometry)
        enc_act = jax.nn.silu(enc_pre).astype(jnp.bfloat16)
        return partial_value + add_rows(shard_rows, receiver_rows, product(enc_act, encoder_outer))

    empty_shard = jnp.zeros((shard_rows, width), jnp.float32)

    def own_block(counter, partial_value):
        return add_block(
            partial_value, local_senders, local_receivers, encoder_features, counter * BLOCK
        )

    enc_partial = lax.fori_loop(0, encoder_counts[0], own_block, empty_shard)
    enc_sum = sent_and_summed(enc_partial.astype(jnp.bfloat16), EDGE, 0)
    node_hidden = jax.nn.silu(
        product(enc_sum.astype(jnp.bfloat16), node_first) + product(mesh_position.T, node_position)
    ).astype(jnp.bfloat16)
    mesh_latent = layer_norm(product(node_hidden, node_second)).astype(jnp.bfloat16)
    receiver_local = mesh_receivers - band_number * shard_rows
    all_latent = whole_of(mesh_latent, MESH_EDGE, (1, 0, 2), 0)
    sender_latent = jnp.take(all_latent, mesh_senders, axis=0)
    receiver_latent = jnp.take(all_latent, mesh_receivers, axis=0)
    proc_pre = (
        product(sender_latent, edge_sender)
        + product(receiver_latent, edge_receiver)
        + product(mesh_features.T, edge_geometry)
    )
    proc_act = jax.nn.silu(proc_pre).astype(jnp.bfloat16)
    proc_partial = add_rows(shard_rows, receiver_local, product(proc_act, edge_outer))
    proc_sum = sent_and_summed(proc_partial.astype(jnp.bfloat16), EDGE, 0).astype(jnp.bfloat16)
    update_pre = product(proc_sum, update_message) + product(mesh_latent, update_state)
    update_act = jax.nn.silu(update_pre).astype(jnp.bfloat16)
    mesh_output = (mesh_latent.astype(jnp.float32) + product(update_act, update_outer)).astype(
        jnp.bfloat16
    )
    grad_pre = (product(cotangent, update_outer.T) * silu_grad(update_pre)).astype(jnp.bfloat16)
    grad_sum = product(grad_pre, update_message.T).astype(jnp.bfloat16)
    grad_node = cotangent.astype(jnp.float32) + product(grad_pre, update_state.T)
    shard_grad = collect(grad_sum, EDGE, 0)
    grad_edge = (
        product(jnp.take(shard_grad, receiver_local, axis=0), edge_outer.T) * silu_grad(proc_pre)
    ).astype(jnp.bfloat16)
    sender_grad = product(grad_edge, edge_sender.T)
    receiver_grad = product(grad_edge, edge_receiver.T)
    total_rows = mesh_rows * lax.axis_size(MESH_EDGE)
    endpoint = add_rows(total_rows, mesh_senders, sender_grad) + add_rows(
        total_rows, mesh_receivers, receiver_grad
    )
    returned = scatter_axes(endpoint, MESH_EDGE, (2, 0, 1), 0)
    return (mesh_output, grad_node + returned)


def solution(mesh):
    split = Mesh(
        mesh.devices.reshape(mesh.shape["groups"], mesh.shape["mesh"], 4, 2),
        ("groups", "mesh", "edge_0", "edge_1"),
    )
    in_specs = (
        P(GROUPS_MESH_EDGE, None),
        P(None, MESH_EDGE),
        P(MESH_EDGE),
        P(MESH_EDGE),
        P(None, MESH_EDGE),
        P(MESH_EDGE),
        P(MESH_EDGE),
        P(MESH_EDGE),
        P(None, MESH_EDGE),
        P(GROUPS_MESH_EDGE, None),
        P(),
        P(),
        P(),
        P(),
        P(),
        P(),
        P(),
        P(),
        P(),
        P(),
        P(),
        P(),
        P(),
        P(),
        P(),
    )
    out_specs = (P(GROUPS_MESH_EDGE, None), P(GROUPS_MESH_EDGE, None))
    return jax.shard_map(
        shards, mesh=split, in_specs=in_specs, out_specs=out_specs, check_vma=False
    )
```

profile of v0, /device:TPU:40, one launch (start us, length us, event | category | flops | bytes accessed | tf_op | source)
XLA Modules:
  0.0 463.8 jit_solution(10006409178802424834)
XLA Ops:
  7.2 1.0 copy-done
  8.2 2.2 fusion.44
  11.0 2.3 broadcast_in_dim.58
  13.4 4.9 %all-to-all-start = ((bf16[8,512,512]{2,1,0:T(8,128)(2,1)}), bf16[8,512,512]{2,1,0:T(8,128)(2,1)}, u32[]{:S(2)}, u32[]{:S(2)}) async-start(bf16[8,512,512]{2,1,0:T(8,128)(2,1)} %broadcast_in_dim.58), calls=%async_computation | async-start | bytes 8388608 | tf_op jit(solution)/shard_map/all_to_all | solution.py:21
  18.4 49.5 %all-to-all-done = bf16[8,512,512]{2,1,0:T(8,128)(2,1)} async-done(((bf16[8,512,512]{2,1,0:T(8,128)(2,1)}), bf16[8,512,512]{2,1,0:T(8,128)(2,1)}, u32[]{:S(2)}, u32[]{:S(2)}) %all-to-all-start) | async-done | bytes 4194336 | tf_op jit(solution)/shard_map/all_to_all | solution.py:21
  67.9 39.8 %while.10 = (s32[]{:T(128)}, f32[128,512]{1,0:T(8,128)S(1)}, s32[]{:T(128)}, s32[2048]{0:T(1024)S(1)}, s32[2048]{0:T(1024)S(1)}, /*index=5*/bf16[4096,512]{1,0:T...) while((s32[]{:T(128)}, f32[128,512]{1,0:T(8,128)S(1)}, ...), condition=%wide.region_3.4_spmd, body=%wide.region_2.3_spmd.sunk | while | flops 235947776 | bytes 3027903 | solution.py:150
  68.8 3.6 gather_fusion
  72.7 1.5 fusion.103
  75.3 3.6 gather_fusion
  79.2 1.5 fusion.103
  81.8 3.6 gather_fusion
  85.7 1.5 fusion.103
  87.2 0.3 convolution_add_fusion.10
  88.3 3.6 gather_fusion
  92.2 1.5 fusion.103
  94.8 3.6 gather_fusion
  98.7 1.5 fusion.103
  100.2 0.3 convolution_add_fusion.10
  101.3 3.6 gather_fusion
  105.2 1.5 fusion.103
  107.7 71.8 %all_to_all.20 = bf16[8,16,512]{2,1,0:T(8,128)(2,1)S(1)} all-to-all(bf16[8,16,512]{2,1,0:T(8,128)(2,1)S(1)} %bitcast.66), channel_id=1, replica_groups=mesh['groups'=2,'mesh'=16,'edge_0'=4,'edge_1'=2] {'edge_0','edge_1'}, dimensions={0} | all-to-all | bytes 262144 | tf_op jit(solution)/shard_map/all_to_all | solution.py:35
  179.8 0.5 fusion.45
  180.5 12.7 %all-gather = bf16[64,512]{1,0:T(8,128)(2,1)} all-gather(bf16[16,512]{1,0:T(8,128)(2,1)S(1)} %multiply_convert_fusion.7), channel_id=2, replica_groups=mesh['groups'=2,'mesh'=16,'edge_0'=4,'edge_1'=2] {'edge_0'}, dimensions={0}, use_global_device_ids=true | all-gather | bytes 81920 | tf_op jit(solution)/shard_map/all_gather | solution.py:42
  193.3 81.3 %all-gather.4.cloned.1.call-done = bf16[64,16,512]{2,1,0:T(8,128)(2,1)} async-done(((bf16[4,16,512]{2,1,0:T(8,128)(2,1)}), bf16[64,16,512]{2,1,0:T(8,128)(2,1)}) %all-gather.4.cloned.1.call-update) | async-done | bytes 1048592 | tf_op jit(solution)/shard_map/all_gather | solution.py:42
  274.8 18.2 %all-gather.6.cloned.1.call-done = bf16[128,16,512]{2,1,0:T(8,128)(2,1)} async-done(((bf16[64,16,512]{2,1,0:T(8,128)(2,1)}), bf16[128,16,512]{2,1,0:T(8,128)(2,1)}) %all-gather.6.cloned.1.call-update) | async-done | bytes 2097168 | tf_op jit(solution)/shard_map/all_gather | solution.py:42
  293.0 1.9 copy.31
  294.9 1.2 gather_fusion.2
  296.1 1.8 gather_fusion.3
  297.9 0.3 fusion.23
  298.3 1.6 convolution_add_fusion.4
  300.2 0.3 fusion.21
  300.5 0.3 convolution_convert_fusion
  301.0 10.2 %all_to_all.21 = bf16[8,16,512]{2,1,0:T(8,128)(2,1)S(1)} all-to-all(bf16[8,16,512]{2,1,0:T(8,128)(2,1)S(1)} %bitcast.67), channel_id=1, replica_groups=mesh['groups'=2,'mesh'=16,'edge_0'=4,'edge_1'=2] {'edge_0','edge_1'}, dimensions={0} | all-to-all | bytes 262144 | tf_op jit(solution)/shard_map/all_to_all | solution.py:35
  312.1 0.7 broadcast_in_dim.61
  312.7 3.6 all-to-all-start.3
  316.6 5.6 %all-to-all-done.3 = bf16[8,16,512]{2,1,0:T(8,128)(2,1)S(1)} async-done(((bf16[8,16,512]{2,1,0:T(8,128)(2,1)}), bf16[8,16,512]{2,1,0:T(8,128)(2,1)S(1)}, u32[]{:S(2)}, u32[]{:S(2)}) %all-to-all-start.3) | async-done | bytes 131104 | tf_op jit(solution)/shard_map/all_to_all | solution.py:21
  322.2 1.2 gather_fusion.1
  323.3 1.6 fusion.14
  324.9 0.3 fusion.50
  325.3 0.3 fusion.51
  325.6 2.0 fusion.13
  327.6 2.1 convolution_add_fusion.2
  329.7 2.4 copy.32
  332.3 20.5 %reduce-scatter.4.cloned.1.call-done = f32[64,16,512]{2,1,0:T(8,128)} async-done(((f32[128,16,512]{2,1,0:T(8,128)}), f32[64,16,512]{2,1,0:T(8,128)}) %reduce-scatter.4.cloned.1.call-update) | async-done | bytes 2097168 | tf_op jit(solution)/shard_map/reduce_scatter | solution.py:59
  352.9 75.9 %reduce-scatter.6.cloned.1.call-done = f32[4,16,512]{2,1,0:T(8,128)} async-done(((f32[64,16,512]{2,1,0:T(8,128)}), f32[4,16,512]{2,1,0:T(8,128)}) %reduce-scatter.6.cloned.1.call-update) | async-done | bytes 131088 | tf_op jit(solution)/shard_map/reduce_scatter | solution.py:59
  428.9 0.8 fusion.16
  429.7 25.9 %reduce-scatter.8.cloned.1.call-done = f32[1,16,512]{2,1,0:T(8,128)} async-done(((f32[4,16,512]{2,1,0:T(8,128)}), f32[1,16,512]{2,1,0:T(8,128)}) %reduce-scatter.8.cloned.1.call-update) | async-done | bytes 32784 | tf_op jit(solution)/shard_map/reduce_scatter | solution.py:59
  455.6 1.6 fusion.15
  (107 shorter events, 7.1 us)
Async XLA Ops:
  7.2 1.0 copy-start
  13.3 5.0 %copy-start.12 = (s32[2048]{0:T(1024)S(1)}, s32[2048]{0:T(1024)}, u32[]{:S(2)}) copy-start(s32[2048]{0:T(1024)} %param.31) | copy-start | bytes 24580
  13.3 5.0 %copy-start.13 = (s32[2048]{0:T(1024)S(1)}, s32[2048]{0:T(1024)}, u32[]{:S(2)}) copy-start(s32[2048]{0:T(1024)} %param.32) | copy-start | bytes 24580
  13.3 54.5 %copy-start.1 = (bf16[512,512]{1,0:T(8,128)(2,1)S(1)}, bf16[512,512]{1,0:T(8,128)(2,1)}, u32[]{:S(2)}) copy-start(bf16[512,512]{1,0:T(8,128)(2,1)} %param.41) | copy-start | bytes 1572868
  13.3 54.5 %copy-start.20 = (bf16[4,512]{1,0:T(4,128)(2,1)S(1)}, bf16[4,512]{1,0:T(4,128)(2,1)}, u32[]{:S(2)}) copy-start(bf16[4,512]{1,0:T(4,128)(2,1)} %param.42) | copy-start | bytes 12292
  13.4 54.5 %all-to-all-start = ((bf16[8,512,512]{2,1,0:T(8,128)(2,1)}), bf16[8,512,512]{2,1,0:T(8,128)(2,1)}, u32[]{:S(2)}, u32[]{:S(2)}) async-start(bf16[8,512,512]{2,1,0:T(8,128)(2,1)} %broadcast_in_dim.58), calls=%async_computation | async-start | bytes 8388608 | tf_op jit(solution)/shard_map/all_to_all | solution.py:21
  18.2 256.4 %all-gather.4.cloned.1.call-start = ((), (), s32[]{:S(2)}) async-start(), calls=%async_computation.7 | async-start | bytes 1114112 | tf_op jit(solution)/shard_map/all_gather | solution.py:42
  67.9 111.7 %copy-start.7 = (bf16[512,512]{1,0:T(8,128)(2,1)S(1)}, bf16[512,512]{1,0:T(8,128)(2,1)}, u32[]{:S(2)}) copy-start(bf16[512,512]{1,0:T(8,128)(2,1)} %param.44) | copy-start | bytes 1572868
  67.9 111.8 %copy-start.8 = (bf16[512,512]{1,0:T(8,128)(2,1)S(1)}, bf16[512,512]{1,0:T(8,128)(2,1)}, u32[]{:S(2)}) copy-start(bf16[512,512]{1,0:T(8,128)(2,1)} %param.46) | copy-start | bytes 1572868
  67.9 111.8 %copy-start.14 = (bf16[3,512]{1,0:T(4,128)(2,1)S(1)}, bf16[3,512]{1,0:T(4,128)(2,1)}, u32[]{:S(2)}) copy-start(bf16[3,512]{1,0:T(4,128)(2,1)} %param.45) | copy-start | bytes 9220
  67.9 111.8 %copy-start.18 = (bf16[3,16]{1,0:T(4,128)(2,1)S(1)}, bf16[3,16]{1,0:T(4,128)(2,1)}, u32[]{:S(2)}) copy-start(bf16[3,16]{1,0:T(4,128)(2,1)} %param.30) | copy-start | bytes 292
  67.9 206.7 %copy-start.16 = (s32[256]{0:T(256)S(1)}, s32[256]{0:T(256)}, u32[]{:S(2)}) copy-start(s32[256]{0:T(256)} %param.35) | copy-start | bytes 3076
  67.9 206.8 %copy-start.11 = (s32[256]{0:T(256)S(1)}, s32[256]{0:T(256)}, u32[]{:S(2)}) copy-start(s32[256]{0:T(256)} %param.36) | copy-start | bytes 3076
  193.2 99.7 %all-gather.6.cloned.1.call-start = ((), (), s32[]{:S(2)}) async-start(), calls=%async_computation.8 | async-start | bytes 3145728 | tf_op jit(solution)/shard_map/all_gather | solution.py:42
  293.0 4.9 %copy-start.2 = (bf16[512,512]{1,0:T(8,128)(2,1)S(1)}, bf16[512,512]{1,0:T(8,128)(2,1)}, u32[]{:S(2)}) copy-start(bf16[512,512]{1,0:T(8,128)(2,1)} %param.47) | copy-start | bytes 1572868
  294.9 5.0 %copy-start.15 = (bf16[4,512]{1,0:T(4,128)(2,1)S(1)}, bf16[4,512]{1,0:T(4,128)(2,1)}, u32[]{:S(2)}) copy-start(bf16[4,512]{1,0:T(4,128)(2,1)} %param.49) | copy-start | bytes 12292
  294.9 5.0 %copy-start.17 = (bf16[4,256]{1,0:T(4,128)(2,1)S(1)}, bf16[4,256]{1,0:T(4,128)(2,1)}, u32[]{:S(2)}) copy-start(bf16[4,256]{1,0:T(4,128)(2,1)} %param.37) | copy-start | bytes 6148
  297.9 2.3 copy-start.19
  297.9 13.3 %copy-start.5 = (bf16[512,512]{1,0:T(8,128)(2,1)S(1)}, bf16[512,512]{1,0:T(8,128)(2,1)}, u32[]{:S(2)}) copy-start(bf16[512,512]{1,0:T(8,128)(2,1)} %param.51) | copy-start | bytes 1572868
  297.9 13.5 %copy-start.4 = (bf16[512,512]{1,0:T(8,128)(2,1)S(1)}, bf16[512,512]{1,0:T(8,128)(2,1)}, u32[]{:S(2)}) copy-start(bf16[512,512]{1,0:T(8,128)(2,1)} %param.52) | copy-start | bytes 1572868
  298.2 13.3 %copy-start.3 = (bf16[512,512]{1,0:T(8,128)(2,1)S(1)}, bf16[512,512]{1,0:T(8,128)(2,1)}, u32[]{:S(2)}) copy-start(bf16[512,512]{1,0:T(8,128)(2,1)} %param.53) | copy-start | bytes 1572868
  298.3 13.3 %copy-start.10 = (bf16[16,512]{1,0:T(8,128)(2,1)S(1)}, bf16[16,512]{1,0:T(8,128)(2,1)}, u32[]{:S(2)}) copy-start(bf16[16,512]{1,0:T(8,128)(2,1)} %param.38) | copy-start | bytes 49156
  300.2 0.8 copy-start.9
  312.0 13.2 %copy-start.6 = (bf16[512,512]{1,0:T(8,128)(2,1)S(1)}, bf16[512,512]{1,0:T(8,128)(2,1)}, u32[]{:S(2)}) copy-start(bf16[512,512]{1,0:T(8,128)(2,1)} %param.48) | copy-start | bytes 1572868
  312.7 9.5 %all-to-all-start.3 = ((bf16[8,16,512]{2,1,0:T(8,128)(2,1)}), bf16[8,16,512]{2,1,0:T(8,128)(2,1)S(1)}, u32[]{:S(2)}, u32[]{:S(2)}) async-start(bf16[8,16,512]{2,1,0:T(8,128)(2,1)} %broadcast_in_dim.61), calls=%async_computation.3 | async-start | bytes 262144 | tf_op jit(solution)/shard_map/all_to_all | solution.py:21
  316.3 36.5 %reduce-scatter.4.cloned.1.call-start = ((), (), s32[]{:S(2)}) async-start(), calls=%async_computation.9 | async-start | bytes 6291456 | tf_op jit(solution)/shard_map/reduce_scatter | solution.py:59
  332.2 96.6 %reduce-scatter.6.cloned.1.call-start = ((), (), s32[]{:S(2)}) async-start(), calls=%async_computation.10 | async-start | bytes 2228224 | tf_op jit(solution)/shard_map/reduce_scatter | solution.py:59
  352.9 102.8 %reduce-scatter.8.cloned.1.call-start = ((), (), s32[]{:S(2)}) async-start(), calls=%async_computation.11 | async-start | bytes 163840 | tf_op jit(solution)/shard_map/reduce_scatter | solution.py:59
Sparse Core Ops, SparseCore 0:
  193.4 81.1 all-gather.3
  276.4 16.5 all-gather.5
  332.3 20.4 reduce-scatter.3
  355.2 73.5 reduce-scatter.5
  431.2 24.3 reduce-scatter.7
where the time goes:
time: 466 us; the launch traced here: 464 us
  waiting for transfers between devices  277 us (59%)
  blocking collectives  94.6 us (20%)
  local copies, waits for them, and re-layouts  35.1 us (8%)
  matrix products  27.6 us (6%)
  between operations  14.3 us (3%)
  starting transfers between devices  8.95 us (2%)
  loops' own time  4.85 us (1%)
    reduce_scatter x3, waiting for transfers between devices, own_block_2(): blocks = lax.psum_scatter(blocks, axes[k], scatter_dimension=0, tiled=True)  122 us
    all_gather x2, waiting for transfers between devices, all_blocks(): blocks = lax.all_gather(blocks, axes[k], axis=0, tiled=True)  99.5 us
    all_to_all x2, blocking collectives, sent_and_summed(): lax.all_to_all(blocks, axis, split_axis=0, concat_axis=0, tiled=True)  81.9 us
    all_to_all x2, waiting for transfers between devices, copy_for_each(): return lax.all_to_all(copies, axis, split_axis=0, concat_axis=0, tiled=True)  55.1 us
    gather x6, local copies, waits for them, and re-layouts, add_block(): enc_pre = product(jnp.take(band_latent, sender_rows, axis=0), encoder_inner)  21.6 us
    dot_general x28, matrix products, product(): return jnp.dot(left, right, preferred_element_type=jnp.float32)  21.3 us
    all_gather x1, blocking collectives, all_blocks(): blocks = lax.all_gather(blocks, axes[k], axis=0, tiled=True)  12.7 us
  transfers between devices with their start and end apart: 7, of which 7 were waited for; matrix products, arithmetic and copies ran while one was open for 0% of the time, Pallas kernels for 0%

commit v1 on v0

v1 whole, which is shorter than its diff:
```python
import functools

import jax
import jax.numpy as jnp
from jax import lax
from jax.experimental import pallas as pl
from jax.experimental.pallas import tpu as pltpu
from jax.sharding import PartitionSpec as P

BLOCK = 128
CHUNK_ROWS = 8
WINDOW = 256
COARSE = 4
MESH = pl.DeviceIdType.MESH
F32 = jnp.float32
BF16 = jnp.bfloat16
I32 = jnp.int32


def bits(size):
    return size.bit_length() - 1


def nn(left, right):
    return jnp.dot(left, right, preferred_element_type=F32)


def nt(left, right):
    return lax.dot_general(left, right, (((1,), (1,)), ((), ())), preferred_element_type=F32)


def tn(left, right):
    return lax.dot_general(left, right, (((0,), (0,)), ((), ())), preferred_element_type=F32)


def tt(left, right):
    return lax.dot_general(left, right, (((0,), (1,)), ((), ())), preferred_element_type=F32)


def sigmoid(values):
    return 0.5 + 0.5 * jnp.tanh(0.5 * values)


def layer_norm(values):
    centred = values - jnp.mean(values, axis=-1, keepdims=True)
    variance = jnp.mean(centred * centred, axis=-1, keepdims=True)
    return centred * lax.rsqrt(variance + 1e-05)


def iota(shape, dim):
    return lax.broadcasted_iota(I32, shape, dim)


def one_hot(hits):
    return jnp.where(hits, 1.0, 0.0).astype(BF16)


def greet(axis, count):
    me = lax.axis_index(axis)
    barrier = pltpu.get_barrier_semaphore()

    def signal(k, carry):
        pl.semaphore_signal(
            barrier, inc=1, device_id={axis: lax.rem(me + k, count)}, device_id_type=MESH
        )
        return carry

    lax.fori_loop(1, count, signal, 0)


def each_peer(axis, count, action):
    me = lax.axis_index(axis)

    def step(k, carry):
        action(me, lax.rem(me + k, count))
        return carry

    lax.fori_loop(1, count, step, 0)


def embed_kernel(
    n_edge,
    count,
    senders,
    receivers,
    features,
    grid_input,
    first,
    second,
    inner,
    packed_all,
    features_all,
    projected,
    rows_v,
    first_v,
    second_v,
    inner_v,
    load_sem,
    send_a,
    send_b,
    recv_a,
    recv_b,
):
    me = lax.axis_index("edge")
    band = lax.axis_index("mesh")
    loads = [
        pltpu.make_async_copy(src, dst, load_sem.at[k])
        for k, (src, dst) in enumerate(
            [(grid_input, rows_v), (first, first_v), (second, second_v), (inner, inner_v)]
        )
    ]
    for load in loads:
        load.start()
    greet("edge", n_edge)
    blocks = senders.shape[0]
    rows = grid_input.shape[0]
    shard = packed_shard(n_edge)
    low = senders[...] - band * (rows * n_edge)
    near = receivers[...] - band * shard
    live = iota((blocks, BLOCK), 0) < count[0]
    packed_all[me] = jnp.where(live, low * shard + near, -1)
    features_all[me] = features[...]
    pl.semaphore_wait(pltpu.get_barrier_semaphore(), n_edge - 1)

    def copy_packed(owner, peer, sem):
        return pltpu.make_async_remote_copy(
            src_ref=packed_all.at[owner],
            dst_ref=packed_all.at[owner],
            send_sem=send_a.at[sem],
            recv_sem=recv_a.at[owner],
            device_id={"edge": peer},
            device_id_type=MESH,
        )

    def copy_features(owner, peer, sem):
        return pltpu.make_async_remote_copy(
            src_ref=features,
            dst_ref=features_all.at[owner],
            send_sem=send_b.at[sem],
            recv_sem=recv_b.at[owner],
            device_id={"edge": peer},
            device_id_type=MESH,
        )

    def send(own, peer):
        copy_packed(own, peer, peer).start()
        copy_features(own, peer, peer).start()

    each_peer("edge", n_edge, send)
    loads[0].wait()
    loads[1].wait()
    hidden = nn(rows_v[...], first_v[...])
    hidden = (hidden * sigmoid(hidden)).astype(BF16)
    loads[2].wait()
    latent = layer_norm(nn(hidden, second_v[...])).astype(BF16)
    loads[3].wait()
    projected[...] = tt(inner_v[...], latent).astype(BF16)

    def arrive(own, peer):
        copy_packed(own, peer, peer).wait_send()
        copy_features(own, peer, peer).wait_send()
        copy_packed(peer, peer, peer).wait_recv()
        copy_features(peer, peer, peer).wait_recv()

    each_peer("edge", n_edge, arrive)


def packed_shard(n_edge):
    return 16 * n_edge


def encode_kernel(
    n_edge,
    shard,
    packed,
    features,
    projected,
    geometry,
    partial,
    position,
    bounds_v,
    bounds,
    queue,
    geometry_v,
    total,
    sem,
):
    me = lax.axis_index("edge")
    blocks = packed.shape[0]
    per_device = blocks // n_edge
    grid_rows = projected.shape[1]
    width = projected.shape[0]
    shift = bits(shard)
    row_bits = bits(grid_rows)
    index = packed[...]
    own = (index >> (shift + row_bits)) == me
    own_b = one_hot(own)
    upper = one_hot(iota((BLOCK, BLOCK), 0) < iota((BLOCK, BLOCK), 1))
    before = one_hot(iota((blocks, blocks), 0) < iota((blocks, blocks), 1))
    lower = one_hot(iota((blocks, blocks), 0) > iota((blocks, blocks), 1))
    ones = jnp.ones((BLOCK, BLOCK), BF16)
    rank = nn(own_b, upper)
    per_block = nn(own_b, ones)
    base = nn(lower, per_block.astype(BF16))
    position[...] = jnp.where(own, (rank + base).astype(I32), -1)
    totals = nt(jnp.ones((8, BLOCK), BF16), own_b)
    starts = nn(totals.astype(BF16), before)
    stops = starts + totals
    bounds_v[...] = jnp.where(iota((8, blocks), 0) == 0, starts, stops).astype(I32)
    copy = pltpu.make_async_copy(bounds_v, bounds, sem)
    copy.start()
    queue[...] = jnp.zeros_like(queue)
    total[...] = jnp.zeros_like(total)
    geometry_v[...] = jnp.zeros_like(geometry_v)
    geometry_v[0:4, :] = geometry[...].astype(F32)
    copy.wait()
    chunk = CHUNK_ROWS * BLOCK
    per_chunk = per_device // CHUNK_ROWS

    def sort_chunk(c, carry):
        first = bounds[0, c * CHUNK_ROWS]
        last = bounds[1, c * CHUNK_ROWS + CHUNK_ROWS - 1]

        @pl.when(last > first)
        def _():
            device = lax.div(c, per_chunk)
            lane = pl.multiple_of(lax.rem(c, per_chunk) * chunk, chunk)
            row = pl.multiple_of(c * CHUNK_ROWS, CHUNK_ROWS)
            code = packed[pl.ds(row, CHUNK_ROWS), :]
            where = position[pl.ds(row, CHUNK_ROWS), :]
            code_row = jnp.concatenate([code[k : k + 1, :] for k in range(CHUNK_ROWS)], axis=1)
            where_row = jnp.concatenate([where[k : k + 1, :] for k in range(CHUNK_ROWS)], axis=1)
            sender = (code_row >> shift) & (grid_rows - 1)
            parts = features[device, :, pl.ds(lane, chunk)].astype(F32)
            parts = jnp.concatenate([parts, jnp.zeros_like(parts)], axis=0)
            place = iota((8, chunk), 0)
            high = (sender >> 7).astype(F32)
            rest = (sender & 127).astype(F32)
            target = ((code_row & (shard - 1)) + 1).astype(F32)
            parts = jnp.where(place == 4, high, parts)
            parts = jnp.where(place == 5, rest, parts)
            parts = jnp.where(place == 6, target, parts)
            parts = parts.astype(BF16)
            start = lax.div(first, BLOCK) * BLOCK

            def fill(w, inner_carry):
                offset = pl.multiple_of(start + w * WINDOW, BLOCK)
                slots = iota((WINDOW, chunk), 0)
                hits = one_hot(slots == where_row - offset)
                queue[:, pl.ds(offset, WINDOW)] += nt(parts, hits)
                return inner_carry

            lax.fori_loop(0, lax.div(last - start + WINDOW - 1, WINDOW), fill, 0)

        return carry

    lax.fori_loop(0, n_edge * per_chunk, sort_chunk, 0)
    found = bounds[1, blocks - 1]

    def encode(j, carry):
        offset = pl.multiple_of(j * WINDOW, WINDOW)
        parts = queue[:, pl.ds(offset, WINDOW)]
        sender = (parts[4:5, :] * 128.0 + parts[5:6, :]).astype(I32)
        target = parts[6:7, :].astype(I32)
        picks = one_hot(iota((grid_rows, WINDOW), 0) == sender)
        goes = one_hot(iota((shard, WINDOW), 0) + 1 == target)
        pre = nn(projected[...], picks)
        pre = pre + tn(geometry_v[...].astype(BF16), parts.astype(BF16))
        act = (pre * sigmoid(pre)).astype(BF16)
        total[...] += nt(goes, act)
        return carry

    lax.fori_loop(0, lax.div(found + WINDOW - 1, WINDOW), encode, 0)
    partial[...] = total[...].astype(BF16)


def step_of(place):
    return jnp.where((place & 1) == 1, (place + 1) >> 1, -(place >> 1))


def place_of(step, n_mesh):
    step = step & (n_mesh - 1)
    return jnp.where(
        step == 0, 0, jnp.where(step <= n_mesh // 2, 2 * step - 1, 2 * (n_mesh - step))
    )


def process_kernel(
    n_mesh,
    n_edge,
    partial,
    mesh_position,
    senders,
    receivers,
    features,
    cotangent,
    node_position,
    geometry,
    w_encoder_outer,
    w_node_first,
    w_node_second,
    w_edge_sender,
    w_edge_receiver,
    w_edge_outer,
    w_update_message,
    w_update_state,
    w_update_outer,
    output,
    gradient,
    encoder_outer,
    node_first,
    node_second,
    edge_sender,
    edge_receiver,
    edge_outer,
    update_message,
    update_state,
    update_outer,
    padded,
    small,
    enc_land,
    latents,
    coarse_own,
    coarse_land,
    coarse,
    send_pick,
    recv_pick,
    send_drop,
    recv_drop,
    edge_term,
    slope,
    proc_send,
    proc_land,
    grads,
    back_band,
    back_band_land,
    back_coarse,
    back_coarse_land,
    back_far,
    back_far_land,
    tail,
    load_sem,
    send_sem,
    recv_sem,
    far_send,
    far_recv,
    relay_send,
    relay_recv,
    final_send,
    final_recv,
):
    me = lax.axis_index("edge")
    band = lax.axis_index("mesh")
    own_rows = cotangent.shape[0]
    shard = own_rows * n_edge
    groups = n_mesh * COARSE // own_rows
    per_group = own_rows // COARSE
    edges = senders.shape[1]
    far_rows = n_mesh * COARSE
    loads = [
        pltpu.make_async_copy(src, dst, load_sem.at[k])
        for k, (src, dst) in enumerate(
            [
                (w_encoder_outer, encoder_outer),
                (w_node_first, node_first),
                (w_node_second, node_second),
                (w_edge_sender, edge_sender),
                (w_edge_receiver, edge_receiver),
                (w_edge_outer, edge_outer),
                (w_update_message, update_message),
                (w_update_state, update_state),
                (w_update_outer, update_outer),
            ]
        )
    ]
    for load in loads:
        load.start()
    greet("edge", n_edge)
    greet("mesh", n_mesh)

    padded[...] = jnp.zeros_like(padded)
    padded[0:3, 0:own_rows] = mesh_position[...].astype(F32)
    place_columns = padded[...].T
    position_term = jnp.zeros((own_rows, node_position.shape[1]), F32)
    for k in range(3):
        position_term += (
            place_columns[0:own_rows, k : k + 1] * node_position[k : k + 1, :].astype(F32)
        )

    pl.semaphore_wait(pltpu.get_barrier_semaphore(), n_edge - 1 + n_mesh - 1)

    def to_peer(phase, src, dst, sem, land):
        def copy(peer):
            return pltpu.make_async_remote_copy(
                src_ref=src(peer),
                dst_ref=dst,
                send_sem=send_sem.at[phase, sem(peer)],
                recv_sem=recv_sem.at[phase, land],
                device_id={"edge": peer},
                device_id_type=MESH,
            )

        return copy

    def start_all(phase, src, dst):
        each_peer(
            "edge",
            n_edge,
            lambda own, peer: to_peer(phase, src, dst.at[own], lambda p: p, own)(peer).start(),
        )

    def wait_all(phase, src, dst):
        def finish(own, peer):
            to_peer(phase, src, dst.at[own], lambda p: p, own)(peer).wait_send()
            to_peer(phase, src, dst.at[peer], lambda p: p, peer)(peer).wait_recv()

        each_peer("edge", n_edge, finish)

    def rows_of(ref):
        return lambda peer: ref.at[pl.ds(pl.multiple_of(peer * own_rows, own_rows), own_rows), :]

    own_slice = pl.ds(pl.multiple_of(me * own_rows, own_rows), own_rows)
    start_all(0, rows_of(partial), enc_land)
    enc_land[me] = partial[own_slice, :]

    sender = senders[...]
    local = sender - band * shard
    owner_band = sender >> bits(shard)
    owner_edge = (sender >> bits(own_rows)) & (n_edge - 1)
    far_place = place_of(owner_band - band, n_mesh)
    far = shard + owner_edge * far_rows + far_place * COARSE + (sender & (COARSE - 1))
    pick = jnp.where(owner_band == band, local, far)
    receiver = receivers[...] - band * shard
    table_rows = shard + n_edge * far_rows
    send_drop[...] = one_hot(iota((table_rows, edges), 0) == pick)
    recv_drop[...] = one_hot(iota((shard, edges), 0) == receiver)
    pick_columns = jnp.broadcast_to(pick.astype(F32), (128, edges)).T.astype(I32)
    recv_columns = jnp.broadcast_to(receiver.astype(F32), (128, edges)).T.astype(I32)
    lanes = iota((edges, 128), 1)
    for k in range(table_rows // 128):
        send_pick[:, k * 128 : (k + 1) * 128] = one_hot(lanes + k * 128 == pick_columns)
    for k in range(shard // 128):
        recv_pick[:, k * 128 : (k + 1) * 128] = one_hot(lanes + k * 128 == recv_columns)
    small[...] = jnp.zeros_like(small)
    small[0:4, 0:edges] = features[...].astype(F32)
    width = geometry.shape[1]
    padded_geometry = jnp.concatenate([geometry[...].astype(F32)] * 2, axis=0)
    padded_geometry = jnp.where(iota((8, width), 0) < 4, padded_geometry, 0.0)
    edge_term[...] = tn(small[...].astype(BF16), padded_geometry.astype(BF16))
    for load in loads:
        load.wait()
    back_out = nt(cotangent[...], update_outer[...])

    wait_all(0, rows_of(partial), enc_land)
    enc_sum = jnp.sum(enc_land[...].astype(F32), axis=0)
    enc_sum = nn(enc_sum.astype(BF16), encoder_outer[...])
    hidden = nn(enc_sum.astype(BF16), node_first[...]) + position_term
    hidden = (hidden * sigmoid(hidden)).astype(BF16)
    latent = layer_norm(nn(hidden, node_second[...])).astype(BF16)
    coarse_own[...] = latent[0:COARSE, :]
    latents[me] = latent

    def far_copy(place, land):
        return pltpu.make_async_remote_copy(
            src_ref=coarse_own,
            dst_ref=coarse_land.at[land],
            send_sem=far_send.at[place],
            recv_sem=far_recv.at[land],
            device_id={"mesh": (band + step_of(place) + n_mesh) & (n_mesh - 1)},
            device_id_type=MESH,
        )

    def far_start(k, carry):
        place = n_mesh - k
        far_copy(place, place_of(-step_of(place), n_mesh)).start()
        return carry

    lax.fori_loop(1, n_mesh, far_start, 0)
    latent_rows = lambda peer: latents.at[me]
    start_all(1, latent_rows, latents)
    coarse_land[0] = coarse_own[...]

    def relay(group, owner, peer):
        return pltpu.make_async_remote_copy(
            src_ref=coarse.at[me, group],
            dst_ref=coarse.at[owner, group],
            send_sem=relay_send.at[group, peer],
            recv_sem=relay_recv.at[group, owner],
            device_id={"edge": peer},
            device_id_type=MESH,
        )

    for group in range(groups):
        for k in range(per_group):
            place = group * per_group + k
            if place > 0:
                far_copy(place, place).wait_recv()
        rows = [coarse_land[group * per_group + k].astype(F32) for k in range(per_group)]
        coarse[me, group] = jnp.concatenate(rows, axis=0).astype(BF16)
        each_peer("edge", n_edge, lambda own, peer: relay(group, own, peer).start())

    wait_all(1, latent_rows, latents)
    band_latent = latents[...].reshape(shard, width)
    recv_rows = nn(recv_pick[...], band_latent).astype(BF16)
    send_rows = nn(send_pick[:, 0:shard], band_latent)
    edge_term[...] += nn(recv_rows, edge_receiver[...])

    def far_finish(k, carry):
        far_copy(k, k).wait_send()
        return carry

    lax.fori_loop(1, n_mesh, far_finish, 0)
    for group in range(groups):

        def relay_finish(own, peer):
            relay(group, own, peer).wait_send()
            relay(group, peer, peer).wait_recv()

        each_peer("edge", n_edge, relay_finish)

    far_latent = coarse[...].reshape(n_edge * far_rows, width)
    send_rows = (send_rows + nn(send_pick[:, shard:], far_latent)).astype(BF16)
    pre = edge_term[...] + nn(send_rows, edge_sender[...])
    sigma = sigmoid(pre)
    act = (pre * sigma).astype(BF16)
    slope[...] = sigma * (1.0 + pre * (1.0 - sigma))
    proc_send[...] = nn(recv_drop[...], act).astype(BF16)
    start_all(2, rows_of(proc_send), proc_land)
    proc_land[me] = proc_send[own_slice, :]
    state_term = nn(latents[me], update_state[...])
    wait_all(2, rows_of(proc_send), proc_land)
    proc_sum = jnp.sum(proc_land[...].astype(F32), axis=0)
    proc_sum = nn(proc_sum.astype(BF16), edge_outer[...]).astype(BF16)
    update_pre = nn(proc_sum, update_message[...]) + state_term
    sigma = sigmoid(update_pre)
    grad_pre = (back_out * (sigma * (1.0 + update_pre * (1.0 - sigma)))).astype(BF16)
    grad_sum = nt(grad_pre, update_message[...]).astype(BF16)
    grads[me] = nt(grad_sum, edge_outer[...]).astype(BF16)
    grad_rows = lambda peer: grads.at[me]
    start_all(3, grad_rows, grads)
    update_act = (update_pre * sigma).astype(BF16)
    mixed = latents[me].astype(F32) + nn(update_act, update_outer[...])
    output[...] = mixed.astype(BF16)
    grad_node = cotangent[...].astype(F32) + nt(grad_pre, update_state[...])
    wait_all(3, grad_rows, grads)
    band_grads = grads[...].reshape(shard, width)
    grad_edge = (nn(recv_pick[...], band_grads) * slope[...]).astype(BF16)
    far_sum = nn(send_drop[shard:, :], grad_edge).astype(BF16)
    back_coarse[...] = far_sum.reshape(n_edge, far_rows, width)
    coarse_rows = lambda peer: back_coarse.at[peer]
    start_all(4, coarse_rows, back_coarse_land)
    back_coarse_land[me] = back_coarse[me]
    to_sender = nn(send_drop[0:shard, :], grad_edge).astype(BF16)
    to_receiver = nn(recv_drop[...], grad_edge).astype(BF16)
    back = nt(to_sender, edge_sender[...]) + nt(to_receiver, edge_receiver[...])
    back_band[...] = back.astype(BF16)
    start_all(5, rows_of(back_band), back_band_land)
    back_band_land[me] = back_band[own_slice, :]
    wait_all(4, coarse_rows, back_coarse_land)
    far_total = jnp.sum(back_coarse_land[...].astype(F32), axis=0)

    def final_copy(place, land):
        return pltpu.make_async_remote_copy(
            src_ref=back_far.at[place],
            dst_ref=back_far_land.at[land],
            send_sem=final_send.at[place],
            recv_sem=final_recv.at[land],
            device_id={"mesh": (band + step_of(place) + n_mesh) & (n_mesh - 1)},
            device_id_type=MESH,
        )

    for place in range(1, n_mesh):
        back_far[place] = far_total[place * COARSE : (place + 1) * COARSE, :].astype(BF16)

    def final_start(k, carry):
        place = n_mesh - k
        final_copy(place, place_of(-step_of(place), n_mesh)).start()
        return carry

    lax.fori_loop(1, n_mesh, final_start, 0)
    wait_all(5, rows_of(back_band), back_band_land)
    result = grad_node + jnp.sum(back_band_land[...].astype(F32), axis=0)

    def final_finish(k, carry):
        final_copy(k, k).wait_send()
        final_copy(k, k).wait_recv()
        return carry

    lax.fori_loop(1, n_mesh, final_finish, 0)
    arrived = back_far_land[1].astype(F32)
    for place in range(2, n_mesh):
        arrived = arrived + back_far_land[place].astype(F32)
    tail[...] = jnp.zeros_like(tail)
    tail[0:COARSE, :] = arrived
    gradient[...] = result + nt(tail[...].astype(BF16), edge_sender[...])


def vmem():
    return pl.BlockSpec(memory_space=pltpu.VMEM)


def anywhere():
    return pl.BlockSpec(memory_space=pl.ANY)


def shards(
    n_mesh,
    n_edge,
    grid_input,
    mesh_position,
    encoder_senders,
    encoder_receivers,
    encoder_features,
    encoder_counts,
    mesh_senders,
    mesh_receivers,
    mesh_features,
    cotangent,
    grid_first,
    grid_second,
    encoder_inner,
    encoder_geometry,
    encoder_outer,
    node_first,
    node_position,
    node_second,
    edge_sender,
    edge_receiver,
    edge_geometry,
    edge_outer,
    update_message,
    update_state,
    update_outer,
):
    grid_rows, channels = grid_input.shape
    width = grid_second.shape[1]
    slots = encoder_senders.shape[0]
    blocks = slots // BLOCK
    own_rows = mesh_position.shape[1]
    shard = own_rows * n_edge
    edges = mesh_senders.shape[0]
    dma = pltpu.SemaphoreType.DMA
    packed, features, projected = pl.pallas_call(
        functools.partial(embed_kernel, n_edge),
        out_shape=(
            jax.ShapeDtypeStruct((n_edge, blocks, BLOCK), I32),
            jax.ShapeDtypeStruct((n_edge, 4, slots), BF16),
            jax.ShapeDtypeStruct((width, grid_rows), BF16),
        ),
        in_specs=[pl.BlockSpec(memory_space=pltpu.SMEM)] + [vmem()] * 3 + [anywhere()] * 4,
        out_specs=(vmem(), vmem(), vmem()),
        scratch_shapes=[
            pltpu.VMEM((grid_rows, channels), BF16),
            pltpu.VMEM((channels, width), BF16),
            pltpu.VMEM((width, width), BF16),
            pltpu.VMEM((width, width), BF16),
            dma((4,)),
            dma((n_edge,)),
            dma((n_edge,)),
            dma((n_edge,)),
            dma((n_edge,)),
        ],
        compiler_params=pltpu.CompilerParams(collective_id=0, has_side_effects=True),
    )(
        encoder_counts,
        encoder_senders.reshape(blocks, BLOCK),
        encoder_receivers.reshape(blocks, BLOCK),
        encoder_features,
        grid_input,
        grid_first,
        grid_second,
        encoder_inner,
    )
    all_blocks = n_edge * blocks
    partial = pl.pallas_call(
        functools.partial(encode_kernel, n_edge, shard),
        out_shape=jax.ShapeDtypeStruct((shard, width), BF16),
        in_specs=[vmem()] * 4,
        out_specs=vmem(),
        scratch_shapes=[
            pltpu.VMEM((all_blocks, BLOCK), I32),
            pltpu.VMEM((8, all_blocks), I32),
            pltpu.SMEM((8, all_blocks), I32),
            pltpu.VMEM((8, n_edge * slots + 2 * WINDOW), F32),
            pltpu.VMEM((8, width), F32),
            pltpu.VMEM((shard, width), F32),
            dma(()),
        ],
    )(packed.reshape(all_blocks, BLOCK), features, projected, encoder_geometry)
    far_rows = n_mesh * COARSE
    groups = far_rows // own_rows
    table_rows = shard + n_edge * far_rows
    weights = [
        encoder_outer,
        node_first,
        node_second,
        edge_sender,
        edge_receiver,
        edge_outer,
        update_message,
        update_state,
        update_outer,
    ]
    return pl.pallas_call(
        functools.partial(process_kernel, n_mesh, n_edge),
        out_shape=(
            jax.ShapeDtypeStruct((own_rows, width), BF16),
            jax.ShapeDtypeStruct((own_rows, width), F32),
        ),
        in_specs=[vmem()] * 8 + [anywhere()] * 9,
        out_specs=(vmem(), vmem()),
        scratch_shapes=[pltpu.VMEM((width, width), BF16) for _ in weights]
        + [
            pltpu.VMEM((128, 128), F32),
            pltpu.VMEM((8, edges), F32),
            pltpu.VMEM((n_edge, own_rows, width), BF16),
            pltpu.VMEM((n_edge, own_rows, width), BF16),
            pltpu.VMEM((COARSE, width), BF16),
            pltpu.VMEM((n_mesh, COARSE, width), BF16),
            pltpu.VMEM((n_edge, groups, own_rows, width), BF16),
            pltpu.VMEM((edges, table_rows), BF16),
            pltpu.VMEM((edges, shard), BF16),
            pltpu.VMEM((table_rows, edges), BF16),
            pltpu.VMEM((shard, edges), BF16),
            pltpu.VMEM((edges, width), F32),
            pltpu.VMEM((edges, width), F32),
            pltpu.VMEM((shard, width), BF16),
            pltpu.VMEM((n_edge, own_rows, width), BF16),
            pltpu.VMEM((n_edge, own_rows, width), BF16),
            pltpu.VMEM((shard, width), BF16),
            pltpu.VMEM((n_edge, own_rows, width), BF16),
            pltpu.VMEM((n_edge, far_rows, width), BF16),
            pltpu.VMEM((n_edge, far_rows, width), BF16),
            pltpu.VMEM((n_mesh, COARSE, width), BF16),
            pltpu.VMEM((n_mesh, COARSE, width), BF16),
            pltpu.VMEM((own_rows, width), F32),
            dma((9,)),
            dma((6, n_edge)),
            dma((6, n_edge)),
            dma((n_mesh,)),
            dma((n_mesh,)),
            dma((groups, n_edge)),
            dma((groups, n_edge)),
            dma((n_mesh,)),
            dma((n_mesh,)),
        ],
        compiler_params=pltpu.CompilerParams(collective_id=1, has_side_effects=True),
    )(
        partial,
        mesh_position,
        mesh_senders.reshape(1, edges),
        mesh_receivers.reshape(1, edges),
        mesh_features,
        cotangent,
        node_position,
        edge_geometry,
        *weights,
    )


def solution(mesh):
    banded = ("mesh", "edge")
    every = ("groups", "mesh", "edge")
    in_specs = (
        P(every, None),
        P(None, banded),
        P(banded),
        P(banded),
        P(None, banded),
        P(banded),
        P(banded),
        P(banded),
        P(None, banded),
        P(every, None),
    ) + (P(),) * 15
    return jax.shard_map(
        functools.partial(shards, mesh.shape["mesh"], mesh.shape["edge"]),
        mesh=mesh,
        in_specs=in_specs,
        out_specs=(P(every, None), P(every, None)),
        check_vma=False,
    )
```

time: 466 us -> 98 us (0.21)
  waiting for transfers between devices: 277 us -> 0 us
  blocking collectives: 94.6 us -> 0 us
  Pallas kernels: 0 us -> 90.9 us
  local copies, waits for them, and re-layouts: 35.1 us -> 3.98 us
  matrix products: 27.6 us -> 0 us
  between operations: 14.3 us -> 1.31 us
  starting transfers between devices: 8.95 us -> 0 us
  loops' own time: 4.85 us -> 0 us
    reduce_scatter x3 -> x0, waiting for transfers between devices: 122 us -> none  [own_block_2(): blocks = lax.psum_scatter(blocks, axes[k], scatter_dimension=0, tiled=True)]
    all_gather x2 -> x0, waiting for transfers between devices: 99.5 us -> none  [all_blocks(): blocks = lax.all_gather(blocks, axes[k], axis=0, tiled=True)]
    pallas_call x0 -> x3, Pallas kernels: none -> 90.9 us  [the longest x1 73.7 us: shards(): pl.pallas_call(functools.partial(process_kernel, n_mesh, n_edge), out_sha...]
    all_to_all x2 -> x0, blocking collectives: 81.9 us -> none  [sent_and_summed(): lax.all_to_all(blocks, axis, split_axis=0, concat_axis=0, tiled=True)]
    all_to_all x2 -> x0, waiting for transfers between devices: 55.1 us -> none  [copy_for_each(): return lax.all_to_all(copies, axis, split_axis=0, concat_axis=0, tiled=True)]
    dot_general x37 -> x0, matrix products: 27.6 us -> none  [the longest x28 21.3 us: product(): return jnp.dot(left, right, preferred_element_type=jnp.float32)]
    gather x9 -> x0, local copies, waits for them, and re-layouts: 25.8 us -> none  [the longest x6 21.6 us: add_block(): enc_pre = product(jnp.take(band_latent, sender_rows, axis=0), encoder_inner)]
    all_gather x1 -> x0, blocking collectives: 12.7 us -> none  [all_blocks(): blocks = lax.all_gather(blocks, axes[k], axis=0, tiled=True)]
  transfers between devices with their start and end apart: 7 -> 0, of which waited for: 7 -> 0; matrix products, arithmetic and copies ran while one was open for 0% -> 0% of each run, Pallas kernels for 0% -> 0%
where the time goes in v1:
time: 98 us; the launch traced here: 96.2 us
  Pallas kernels  90.9 us (93%)
  local copies, waits for them, and re-layouts  3.98 us (4%)
  between operations  1.31 us (1%)
    pallas_call x1, Pallas kernels, shards(): pl.pallas_call(functools.partial(process_kernel, n_mesh, n_edge), out_sha...  73.7 us
    pallas_call x1, Pallas kernels, shards(): pl.pallas_call(functools.partial(embed_kernel, n_edge), out_shape=(jax.Sh...  9.38 us
    pallas_call x1, Pallas kernels, shards(): pl.pallas_call(functools.partial(encode_kernel, n_edge, shard), out_shape...  7.76 us
    unnamed x5, local copies, waits for them, and re-layouts  3.98 us

profile of v1, /device:TPU:40, one launch (start us, length us, event | category | flops | bytes accessed | tf_op | source)
XLA Modules:
  0.0 96.2 jit_solution(14008203449830027237)
XLA Ops:
  1.3 2.0 %copy.27.grid_input = bf16[512,474]{1,0:T(8,128)(2,1)} copy(bf16[512,474]{0,1:T(8,128)(2,1)} %param.25) | data formatting | bytes 970752 | tf_op args[0]
  3.3 9.4 %shard_map.248 = (s32[8,16,128]{2,1,0:T(8,128)}, bf16[8,4,2048]{2,1,0:T(4,128)(2,1)}, bf16[512,512]{1,0:T(8,128)(2,1)}) custom-call(s32[1]{0:T(128)S(6)} %copy.30.count, s32[16,128]{1,0:T(8,128)} %bitcast.6, s32[16,128]{1,0:T(8,128)} %bitcast.7, bf16[4,2048]{1,0:T(4,128)(2,1)} %features.2, bf16[512,474]{1,0:T(8,128)(2,1)} %copy.27.grid_input, ...), custom_call_target="tpu_custom_call" | custom-call | tf_op jit(solution)/shard_map/pallas_call | solution.py:643
  12.7 7.8 %shard_map.249.partial = bf16[128,512]{1,0:T(8,128)(2,1)} custom-call(s32[128,128]{1,0:T(8,128)} %bitcast.5, bf16[8,4,2048]{2,1,0:T(4,128)(2,1)} %get-tuple-element.6.features, bf16[512,512]{1,0:T(8,128)(2,1)} %get-tuple-element.7.projected, bf16[4,512]{1,0:T(4,128)(2,1)} %geometry.2), custom_call_target="tpu_custom_call" | custom-call | tf_op jit(solution)/shard_map/pallas_call | solution.py:675
  20.5 73.7 %shard_map.250 = (bf16[16,512]{1,0:T(8,128)(2,1)}, f32[16,512]{1,0:T(8,128)}) custom-call(bf16[128,512]{1,0:T(8,128)(2,1)} %shard_map.249.partial, bf16[3,16]{1,0:T(4,128)(2,1)} %mesh_position.1, s32[1,256]{1,0:T(1,128)} %bitcast.8, s32[1,256]{1,0:T(1,128)} %bitcast.9, bf16[4,256]{1,0:T(4,128)(2,1)} %features.3, bf16[16,512]{1,0:T(8,128)(2,1)} %cotangent.1, ...), custom_call_target="tpu_custom_call" | custom-call | tf_op jit(solution)/shard_map/pallas_call | solution.py:704
  94.2 0.0 copy-start
  94.2 1.3 %copy.31 = bf16[16,512]{1,0:T(8,128)(2,1)} copy(bf16[16,512]{1,0:T(8,128)(2,1)} %get-tuple-element.10) | data formatting | bytes 32768
  95.6 0.0 copy-done
  95.6 0.6 copy.32
Async XLA Ops:
  94.2 1.3 %copy-start = (f32[16,512]{1,0:T(8,128)S(1)}, f32[16,512]{1,0:T(8,128)}, u32[]{:S(2)}) copy-start(f32[16,512]{1,0:T(8,128)} %get-tuple-element.11) | copy-start | bytes 98308

commit v2 on v1

--- a/solution.py
+++ b/solution.py
@@ -10,6 +10,7 @@
 BLOCK = 128
 CHUNK_ROWS = 8
 WINDOW = 256
+STEP = 512
 COARSE = 4
 MESH = pl.DeviceIdType.MESH
 F32 = jnp.float32
@@ -84,6 +85,9 @@
     senders,
     receivers,
     features,
+    mesh_senders,
+    mesh_receivers,
+    mesh_features,
     grid_input,
     first,
     second,
@@ -91,6 +95,11 @@
     packed_all,
     features_all,
     projected,
+    pair_senders,
+    pair_receivers,
+    pair_features,
+    senders_v,
+    receivers_v,
     rows_v,
     first_v,
     second_v,
@@ -100,26 +109,43 @@
     send_b,
     recv_a,
     recv_b,
+    pair_send,
+    pair_recv,
 ):
     me = lax.axis_index("edge")
     band = lax.axis_index("mesh")
+    core = me & 1
     loads = [
         pltpu.make_async_copy(src, dst, load_sem.at[k])
         for k, (src, dst) in enumerate(
-            [(grid_input, rows_v), (first, first_v), (second, second_v), (inner, inner_v)]
+            [
+                (senders, senders_v),
+                (receivers, receivers_v),
+                (features, features_all.at[me]),
+                (mesh_senders, pair_senders.at[core]),
+                (mesh_receivers, pair_receivers.at[core]),
+                (mesh_features, pair_features.at[core]),
+                (grid_input, rows_v),
+                (first, first_v),
+                (second, second_v),
+                (inner, inner_v),
+            ]
         )
     ]
     for load in loads:
         load.start()
     greet("edge", n_edge)
     blocks = senders.shape[0]
-    rows = grid_input.shape[0]
+    rows = grid_input.shape[1]
     shard = packed_shard(n_edge)
-    low = senders[...] - band * (rows * n_edge)
-    near = receivers[...] - band * shard
+    loads[0].wait()
+    loads[1].wait()
+    low = senders_v[...] - band * (rows * n_edge)
+    near = receivers_v[...] - band * shard
     live = iota((blocks, BLOCK), 0) < count[0]
     packed_all[me] = jnp.where(live, low * shard + near, -1)
-    features_all[me] = features[...]
+    for load in loads[2:6]:
+        load.wait()
     pl.semaphore_wait(pltpu.get_barrier_semaphore(), n_edge - 1)
 
     def copy_packed(owner, peer, sem):
@@ -134,7 +160,7 @@
 
     def copy_features(owner, peer, sem):
         return pltpu.make_async_remote_copy(
-            src_ref=features,
+            src_ref=features_all.at[owner],
             dst_ref=features_all.at[owner],
             send_sem=send_b.at[sem],
             recv_sem=recv_b.at[owner],
@@ -147,13 +173,27 @@
         copy_features(own, peer, peer).start()
 
     each_peer("edge", n_edge, send)
-    loads[0].wait()
-    loads[1].wait()
-    hidden = nn(rows_v[...], first_v[...])
+
+    def copy_pair(ref, slot, k):
+        return pltpu.make_async_remote_copy(
+            src_ref=ref.at[slot],
+            dst_ref=ref.at[slot],
+            send_sem=pair_send.at[k],
+            recv_sem=pair_recv.at[k],
+            device_id={"edge": me ^ 1},
+            device_id_type=MESH,
+        )
+
+    pairs = (pair_senders, pair_receivers, pair_features)
+    for k, ref in enumerate(pairs):
+        copy_pair(ref, core, k).start()
+    loads[6].wait()
+    loads[7].wait()
+    hidden = tn(rows_v[...], first_v[...])
     hidden = (hidden * sigmoid(hidden)).astype(BF16)
-    loads[2].wait()
+    loads[8].wait()
     latent = layer_norm(nn(hidden, second_v[...])).astype(BF16)
-    loads[3].wait()
+    loads[9].wait()
     projected[...] = tt(inner_v[...], latent).astype(BF16)
 
     def arrive(own, peer):
@@ -163,6 +203,9 @@
         copy_features(peer, peer, peer).wait_recv()
 
     each_peer("edge", n_edge, arrive)
+    for k, ref in enumerate(pairs):
+        copy_pair(ref, core, k).wait_send()
+        copy_pair(ref, core ^ 1, k).wait_recv()
 
 
 def packed_shard(n_edge):
@@ -182,10 +225,14 @@
     bounds,
     queue,
     geometry_v,
+    geometry_w,
     total,
     sem,
+    geometry_sem,
 ):
     me = lax.axis_index("edge")
+    load = pltpu.make_async_copy(geometry, geometry_w, geometry_sem)
+    load.start()
     blocks = packed.shape[0]
     per_device = blocks // n_edge
     grid_rows = projected.shape[1]
@@ -212,65 +259,74 @@
     queue[...] = jnp.zeros_like(queue)
     total[...] = jnp.zeros_like(total)
     geometry_v[...] = jnp.zeros_like(geometry_v)
-    geometry_v[0:4, :] = geometry[...].astype(F32)
     copy.wait()
     chunk = CHUNK_ROWS * BLOCK
     per_chunk = per_device // CHUNK_ROWS
 
+    def chunk_of(c, device, lane, row):
+        code = packed[pl.ds(row, CHUNK_ROWS), :]
+        where = position[pl.ds(row, CHUNK_ROWS), :]
+        code_row = jnp.concatenate([code[k : k + 1, :] for k in range(CHUNK_ROWS)], axis=1)
+        where_row = jnp.concatenate([where[k : k + 1, :] for k in range(CHUNK_ROWS)], axis=1)
+        sender = (code_row >> shift) & (grid_rows - 1)
+        parts = features[device, :, pl.ds(lane, chunk)].astype(F32)
+        parts = jnp.concatenate([parts, jnp.zeros_like(parts)], axis=0)
+        place = iota((8, chunk), 0)
+        parts = jnp.where(place == 4, (sender >> 7).astype(F32), parts)
+        parts = jnp.where(place == 5, (sender & 127).astype(F32), parts)
+        parts = jnp.where(place == 6, ((code_row & (shard - 1)) + 1).astype(F32), parts)
+        return parts.astype(BF16), where_row
+
+    def fill(parts, where_row, offset):
+        offset = pl.multiple_of(offset, BLOCK)
+        hits = one_hot(iota((WINDOW, chunk), 0) == where_row - offset)
+        queue[:, pl.ds(offset, WINDOW)] += nt(parts, hits)
+
+    for device in range(n_edge):
+        c = device * per_chunk
+        parts, where_row = chunk_of(c, device, 0, c * CHUNK_ROWS)
+        fill(parts, where_row, bounds[0, c * CHUNK_ROWS] & -BLOCK)
+
     def sort_chunk(c, carry):
         first = bounds[0, c * CHUNK_ROWS]
         last = bounds[1, c * CHUNK_ROWS + CHUNK_ROWS - 1]
-
-        @pl.when(last > first)
+        part = c & (per_chunk - 1)
+        skip = jnp.where(part == 0, WINDOW, 0)
+        start = (first & -BLOCK) + skip
+
+        @pl.when((last > first) & (last > start))
         def _():
-            device = lax.div(c, per_chunk)
-            lane = pl.multiple_of(lax.rem(c, per_chunk) * chunk, chunk)
+            lane = pl.multiple_of(part * chunk, chunk)
             row = pl.multiple_of(c * CHUNK_ROWS, CHUNK_ROWS)
-            code = packed[pl.ds(row, CHUNK_ROWS), :]
-            where = position[pl.ds(row, CHUNK_ROWS), :]
-            code_row = jnp.concatenate([code[k : k + 1, :] for k in range(CHUNK_ROWS)], axis=1)
-            where_row = jnp.concatenate([where[k : k + 1, :] for k in range(CHUNK_ROWS)], axis=1)
-            sender = (code_row >> shift) & (grid_rows - 1)
-            parts = features[device, :, pl.ds(lane, chunk)].astype(F32)
-            parts = jnp.concatenate([parts, jnp.zeros_like(parts)], axis=0)
-            place = iota((8, chunk), 0)
-            high = (sender >> 7).astype(F32)
-            rest = (sender & 127).astype(F32)
-            target = ((code_row & (shard - 1)) + 1).astype(F32)
-            parts = jnp.where(place == 4, high, parts)
-            parts = jnp.where(place == 5, rest, parts)
-            parts = jnp.where(place == 6, target, parts)
-            parts = parts.astype(BF16)
-            start = lax.div(first, BLOCK) * BLOCK
-
-            def fill(w, inner_carry):
-                offset = pl.multiple_of(start + w * WINDOW, BLOCK)
-                slots = iota((WINDOW, chunk), 0)
-                hits = one_hot(slots == where_row - offset)
-                queue[:, pl.ds(offset, WINDOW)] += nt(parts, hits)
+            parts, where_row = chunk_of(c, c >> bits(per_chunk), lane, row)
+
+            def more(w, inner_carry):
+                fill(parts, where_row, start + w * WINDOW)
                 return inner_carry
 
-            lax.fori_loop(0, lax.div(last - start + WINDOW - 1, WINDOW), fill, 0)
+            lax.fori_loop(0, (last - start + WINDOW - 1) >> bits(WINDOW), more, 0)
 
         return carry
 
     lax.fori_loop(0, n_edge * per_chunk, sort_chunk, 0)
+    load.wait()
+    geometry_v[0:4, :] = geometry_w[...].astype(F32)
     found = bounds[1, blocks - 1]
 
     def encode(j, carry):
-        offset = pl.multiple_of(j * WINDOW, WINDOW)
-        parts = queue[:, pl.ds(offset, WINDOW)]
+        offset = pl.multiple_of(j * STEP, STEP)
+        parts = queue[:, pl.ds(offset, STEP)]
         sender = (parts[4:5, :] * 128.0 + parts[5:6, :]).astype(I32)
         target = parts[6:7, :].astype(I32)
-        picks = one_hot(iota((grid_rows, WINDOW), 0) == sender)
-        goes = one_hot(iota((shard, WINDOW), 0) + 1 == target)
+        picks = one_hot(iota((grid_rows, STEP), 0) == sender)
+        goes = one_hot(iota((shard, STEP), 0) + 1 == target)
         pre = nn(projected[...], picks)
         pre = pre + tn(geometry_v[...].astype(BF16), parts.astype(BF16))
         act = (pre * sigmoid(pre)).astype(BF16)
         total[...] += nt(goes, act)
         return carry
 
-    lax.fori_loop(0, lax.div(found + WINDOW - 1, WINDOW), encode, 0)
+    lax.fori_loop(0, lax.div(found + STEP - 1, STEP), encode, 0)
     partial[...] = total[...].astype(BF16)
 
 
@@ -290,9 +346,9 @@
     n_edge,
     partial,
     mesh_position,
-    senders,
-    receivers,
-    features,
+    pair_senders,
+    pair_receivers,
+    pair_features,
     cotangent,
     node_position,
     geometry,
@@ -339,6 +395,8 @@
     back_far,
     back_far_land,
     tail,
+    enc_node,
+    edge_update,
     load_sem,
     send_sem,
     recv_sem,
@@ -346,6 +404,7 @@
     far_recv,
     relay_send,
     relay_recv,
+    forward_send,
     final_send,
     final_recv,
 ):
@@ -355,7 +414,7 @@
     shard = own_rows * n_edge
     groups = n_mesh * COARSE // own_rows
     per_group = own_rows // COARSE
-    edges = senders.shape[1]
+    edges = 2 * pair_senders.shape[2]
     far_rows = n_mesh * COARSE
     loads = [
         pltpu.make_async_copy(src, dst, load_sem.at[k])
@@ -389,6 +448,18 @@
 
     pl.semaphore_wait(pltpu.get_barrier_semaphore(), n_edge - 1 + n_mesh - 1)
 
+    core = me & 1
+    chip = me >> 1
+    chips = n_edge // 2
+    chip_rows = chips * own_rows
+
+    def each_chip(action):
+        def step(k, carry):
+            action(((chip + k) & (chips - 1)) * 2 + core)
+            return carry
+
+        lax.fori_loop(1, chips, step, 0)
+
     def to_peer(phase, src, dst, sem, land):
         def copy(peer):
             return pltpu.make_async_remote_copy(
@@ -416,6 +487,28 @@
 
         each_peer("edge", n_edge, finish)
 
+    def chip_all(phase, ref, land, rows):
+        def copy(peer, slot):
+            start = pl.multiple_of((peer >> 1) * rows, rows)
+            return pltpu.make_async_remote_copy(
+                src_ref=ref.at[pl.ds(start, rows), :],
+                dst_ref=land.at[slot],
+                send_sem=send_sem.at[phase, peer],
+                recv_sem=recv_sem.at[phase, slot],
+                device_id={"edge": peer},
+                device_id_type=MESH,
+            )
+
+        def start():
+            each_chip(lambda peer: copy(peer, chip).start())
+            land[chip] = ref[pl.ds(pl.multiple_of(chip * rows, rows), rows), :]
+
+        def finish():
+            each_chip(lambda peer: copy(peer, chip).wait_send())
+            each_chip(lambda peer: copy(peer, peer >> 1).wait_recv())
+
+        return start, finish
+
     def rows_of(ref):
         return lambda peer: ref.at[pl.ds(pl.multiple_of(peer * own_rows, own_rows), own_rows), :]
 
@@ -423,17 +516,29 @@
     start_all(0, rows_of(partial), enc_land)
     enc_land[me] = partial[own_slice, :]
 
-    sender = senders[...]
-    local = sender - band * shard
+    sender = jnp.concatenate([pair_senders[0], pair_senders[1]], axis=1)
+    receiver = jnp.concatenate([pair_receivers[0], pair_receivers[1]], axis=1)
     owner_band = sender >> bits(shard)
+    near = owner_band == band
     owner_edge = (sender >> bits(own_rows)) & (n_edge - 1)
     far_place = place_of(owner_band - band, n_mesh)
-    far = shard + owner_edge * far_rows + far_place * COARSE + (sender & (COARSE - 1))
-    pick = jnp.where(owner_band == band, local, far)
-    receiver = receivers[...] - band * shard
+    far_row = far_place * COARSE + (sender & (COARSE - 1))
+    local = sender - band * shard
+    pick = jnp.where(near, local, shard + owner_edge * far_rows + far_row)
+    receiver = receiver - band * shard
     table_rows = shard + n_edge * far_rows
-    send_drop[...] = one_hot(iota((table_rows, edges), 0) == pick)
-    recv_drop[...] = one_hot(iota((shard, edges), 0) == receiver)
+
+    def chip_row(row, owner):
+        own_core = (owner & 1) == core
+        return jnp.where(own_core, (owner >> 1) * own_rows + (row & (own_rows - 1)), -1)
+
+    drop_near = jnp.where(near, chip_row(local, owner_edge), -1)
+    drop_far = jnp.where((owner_edge & 1) == core, (owner_edge >> 1) * far_rows + far_row, -1)
+    drop_far = jnp.where(near, -1, drop_far)
+    drop_recv = chip_row(receiver, receiver >> bits(own_rows))
+    send_drop[0:chip_rows, :] = one_hot(iota((chip_rows, edges), 0) == drop_near)
+    send_drop[chip_rows:, :] = one_hot(iota((chips * far_rows, edges), 0) == drop_far)
+    recv_drop[...] = one_hot(iota((chip_rows, edges), 0) == drop_recv)
     pick_columns = jnp.broadcast_to(pick.astype(F32), (128, edges)).T.astype(I32)
     recv_columns = jnp.broadcast_to(receiver.astype(F32), (128, edges)).T.astype(I32)
     lanes = iota((edges, 128), 1)
@@ -442,7 +547,9 @@
     for k in range(shard // 128):
         recv_pick[:, k * 128 : (k + 1) * 128] = one_hot(lanes + k * 128 == recv_columns)
     small[...] = jnp.zeros_like(small)
-    small[0:4, 0:edges] = features[...].astype(F32)
+    half = edges // 2
+    small[0:4, 0:half] = pair_features[0].astype(F32)
+    small[0:4, half:edges] = pair_features[1].astype(F32)
     width = geometry.shape[1]
     padded_geometry = jnp.concatenate([geometry[...].astype(F32)] * 2, axis=0)
     padded_geometry = jnp.where(iota((8, width), 0) < 4, padded_geometry, 0.0)
@@ -450,11 +557,11 @@
     for load in loads:
         load.wait()
     back_out = nt(cotangent[...], update_outer[...])
+    enc_node[...] = nn(encoder_outer[...], node_first[...]).astype(BF16)
 
     wait_all(0, rows_of(partial), enc_land)
     enc_sum = jnp.sum(enc_land[...].astype(F32), axis=0)
-    enc_sum = nn(enc_sum.astype(BF16), encoder_outer[...])
-    hidden = nn(enc_sum.astype(BF16), node_first[...]) + position_term
+    hidden = nn(enc_sum.astype(BF16), enc_node[...]) + position_term
     hidden = (hidden * sigmoid(hidden)).astype(BF16)
     latent = layer_norm(nn(hidden, node_second[...])).astype(BF16)
     coarse_own[...] = latent[0:COARSE, :]
@@ -482,13 +589,30 @@
 
     def relay(group, owner, peer):
         return pltpu.make_async_remote_copy(
-            src_ref=coarse.at[me, group],
+            src_ref=coarse.at[owner, group],
             dst_ref=coarse.at[owner, group],
             send_sem=relay_send.at[group, peer],
             recv_sem=relay_recv.at[group, owner],
             device_id={"edge": peer},
             device_id_type=MESH,
         )
+
+    def forward(group, owner):
+        return pltpu.make_async_remote_copy(
+            src_ref=coarse.at[owner, group],
+            dst_ref=coarse.at[owner, group],
+            send_sem=forward_send.at[group, owner],
+            recv_sem=relay_recv.at[group, owner],
+            device_id={"edge": me ^ 1},
+            device_id_type=MESH,
+        )
+
+    def pass_on(group):
+        def step(owner):
+            relay(group, owner, owner).wait_recv()
+            forward(group, owner).start()
+
+        each_chip(step)
 
     for group in range(groups):
         for k in range(per_group):
@@ -497,8 +621,13 @@
                 far_copy(place, place).wait_recv()
         rows = [coarse_land[group * per_group + k].astype(F32) for k in range(per_group)]
         coarse[me, group] = jnp.concatenate(rows, axis=0).astype(BF16)
-        each_peer("edge", n_edge, lambda own, peer: relay(group, own, peer).start())
-
+        each_chip(lambda peer: relay(group, me, peer).start())
+        relay(group, me, me ^ 1).start()
+        if group > 0:
+            pass_on(group - 1)
+    pass_on(groups - 1)
+
+    edge_update[...] = nn(edge_outer[...], update_message[...]).astype(BF16)
     wait_all(1, latent_rows, latents)
     band_latent = latents[...].reshape(shard, width)
     recv_rows = nn(recv_pick[...], band_latent).astype(BF16)
@@ -512,11 +641,14 @@
     lax.fori_loop(1, n_mesh, far_finish, 0)
     for group in range(groups):
 
-        def relay_finish(own, peer):
-            relay(group, own, peer).wait_send()
-            relay(group, peer, peer).wait_recv()
-
-        each_peer("edge", n_edge, relay_finish)
+        def relay_finish(peer):
+            relay(group, me, peer).wait_send()
+            forward(group, peer).wait_send()
+            forward(group, peer ^ 1).wait_recv()
+
+        each_chip(relay_finish)
+        relay(group, me, me ^ 1).wait_send()
+        relay(group, me ^ 1, me).wait_recv()
 
     far_latent = coarse[...].reshape(n_edge * far_rows, width)
     send_rows = (send_rows + nn(send_pick[:, shard:], far_latent)).astype(BF16)
@@ -525,17 +657,15 @@
     act = (pre * sigma).astype(BF16)
     slope[...] = sigma * (1.0 + pre * (1.0 - sigma))
     proc_send[...] = nn(recv_drop[...], act).astype(BF16)
-    start_all(2, rows_of(proc_send), proc_land)
-    proc_land[me] = proc_send[own_slice, :]
+    proc_start, proc_finish = chip_all(2, proc_send, proc_land, own_rows)
+    proc_start()
     state_term = nn(latents[me], update_state[...])
-    wait_all(2, rows_of(proc_send), proc_land)
+    proc_finish()
     proc_sum = jnp.sum(proc_land[...].astype(F32), axis=0)
-    proc_sum = nn(proc_sum.astype(BF16), edge_outer[...]).astype(BF16)
-    update_pre = nn(proc_sum, update_message[...]) + state_term
+    update_pre = nn(proc_sum.astype(BF16), edge_update[...]) + state_term
     sigma = sigmoid(update_pre)
     grad_pre = (back_out * (sigma * (1.0 + update_pre * (1.0 - sigma)))).astype(BF16)
-    grad_sum = nt(grad_pre, update_message[...]).astype(BF16)
-    grads[me] = nt(grad_sum, edge_outer[...]).astype(BF16)
+    grads[me] = nt(grad_pre, edge_update[...]).astype(BF16)
     grad_rows = lambda peer: grads.at[me]
     start_all(3, grad_rows, grads)
     update_act = (update_pre * sigma).astype(BF16)
@@ -545,18 +675,16 @@
     wait_all(3, grad_rows, grads)
     band_grads = grads[...].reshape(shard, width)
     grad_edge = (nn(recv_pick[...], band_grads) * slope[...]).astype(BF16)
-    far_sum = nn(send_drop[shard:, :], grad_edge).astype(BF16)
-    back_coarse[...] = far_sum.reshape(n_edge, far_rows, width)
-    coarse_rows = lambda peer: back_coarse.at[peer]
-    start_all(4, coarse_rows, back_coarse_land)
-    back_coarse_land[me] = back_coarse[me]
-    to_sender = nn(send_drop[0:shard, :], grad_edge).astype(BF16)
+    back_coarse[...] = nn(send_drop[chip_rows:, :], grad_edge).astype(BF16)
+    coarse_start, coarse_finish = chip_all(4, back_coarse, back_coarse_land, far_rows)
+    coarse_start()
+    to_sender = nn(send_drop[0:chip_rows, :], grad_edge).astype(BF16)
     to_receiver = nn(recv_drop[...], grad_edge).astype(BF16)
     back = nt(to_sender, edge_sender[...]) + nt(to_receiver, edge_receiver[...])
     back_band[...] = back.astype(BF16)
-    start_all(5, rows_of(back_band), back_band_land)
-    back_band_land[me] = back_band[own_slice, :]
-    wait_all(4, coarse_rows, back_coarse_land)
+    band_start, band_finish = chip_all(5, back_band, back_band_land, own_rows)
+    band_start()
+    coarse_finish()
     far_total = jnp.sum(back_coarse_land[...].astype(F32), axis=0)
 
     def final_copy(place, land):
@@ -578,7 +706,7 @@
         return carry
 
     lax.fori_loop(1, n_mesh, final_start, 0)
-    wait_all(5, rows_of(back_band), back_band_land)
+    band_finish()
     result = grad_node + jnp.sum(back_band_land[...].astype(F32), axis=0)
 
     def final_finish(k, carry):
@@ -595,12 +723,21 @@
     gradient[...] = result + nt(tail[...].astype(BF16), edge_sender[...])
 
 
+def finish_kernel(output, gradient, output_copy, gradient_copy):
+    output_copy[...] = output[...]
+    gradient_copy[...] = gradient[...]
+
+
 def vmem():
     return pl.BlockSpec(memory_space=pltpu.VMEM)
 
 
 def anywhere():
-    return pl.BlockSpec(memory_space=pl.ANY)
+    return pl.BlockSpec(memory_space=pltpu.HBM)
+
+
+def hbm(value):
+    return pltpu.with_memory_space_constraint(value, pltpu.HBM)
 
 
 def shards(
@@ -640,56 +777,73 @@
     shard = own_rows * n_edge
     edges = mesh_senders.shape[0]
     dma = pltpu.SemaphoreType.DMA
-    packed, features, projected = pl.pallas_call(
+    packed, features, projected, pair_senders, pair_receivers, pair_features = pl.pallas_call(
         functools.partial(embed_kernel, n_edge),
         out_shape=(
             jax.ShapeDtypeStruct((n_edge, blocks, BLOCK), I32),
             jax.ShapeDtypeStruct((n_edge, 4, slots), BF16),
             jax.ShapeDtypeStruct((width, grid_rows), BF16),
+            jax.ShapeDtypeStruct((2, 1, edges), I32),
+            jax.ShapeDtypeStruct((2, 1, edges), I32),
+            jax.ShapeDtypeStruct((2, 4, edges), BF16),
         ),
-        in_specs=[pl.BlockSpec(memory_space=pltpu.SMEM)] + [vmem()] * 3 + [anywhere()] * 4,
-        out_specs=(vmem(), vmem(), vmem()),
+        in_specs=[pl.BlockSpec(memory_space=pltpu.SMEM)] + [anywhere()] * 10,
+        out_specs=(vmem(),) * 6,
         scratch_shapes=[
-            pltpu.VMEM((grid_rows, channels), BF16),
+            pltpu.VMEM((blocks, BLOCK), I32),
+            pltpu.VMEM((blocks, BLOCK), I32),
+            pltpu.VMEM((channels, grid_rows), BF16),
             pltpu.VMEM((channels, width), BF16),
             pltpu.VMEM((width, width), BF16),
             pltpu.VMEM((width, width), BF16),
-            dma((4,)),
+            dma((10,)),
             dma((n_edge,)),
             dma((n_edge,)),
             dma((n_edge,)),
             dma((n_edge,)),
+            dma((3,)),
+            dma((3,)),
         ],
-        compiler_params=pltpu.CompilerParams(collective_id=0, has_side_effects=True),
+        compiler_params=pltpu.CompilerParams(
+            collective_id=0, has_side_effects=True, vmem_limit_bytes=12 << 20
+        ),
     )(
         encoder_counts,
-        encoder_senders.reshape(blocks, BLOCK),
-        encoder_receivers.reshape(blocks, BLOCK),
-        encoder_features,
-        grid_input,
-        grid_first,
-        grid_second,
-        encoder_inner,
+        hbm(encoder_senders.reshape(blocks, BLOCK)),
+        hbm(encoder_receivers.reshape(blocks, BLOCK)),
+        hbm(encoder_features),
+        hbm(mesh_senders.reshape(1, edges)),
+        hbm(mesh_receivers.reshape(1, edges)),
+        hbm(mesh_features),
+        hbm(grid_input.T),
+        hbm(grid_first),
+        hbm(grid_second),
+        hbm(encoder_inner),
     )
     all_blocks = n_edge * blocks
     partial = pl.pallas_call(
         functools.partial(encode_kernel, n_edge, shard),
         out_shape=jax.ShapeDtypeStruct((shard, width), BF16),
-        in_specs=[vmem()] * 4,
+        in_specs=[vmem()] * 3 + [anywhere()],
         out_specs=vmem(),
         scratch_shapes=[
             pltpu.VMEM((all_blocks, BLOCK), I32),
             pltpu.VMEM((8, all_blocks), I32),
             pltpu.SMEM((8, all_blocks), I32),
-            pltpu.VMEM((8, n_edge * slots + 2 * WINDOW), F32),
+            pltpu.VMEM((8, n_edge * slots + STEP), F32),
             pltpu.VMEM((8, width), F32),
+            pltpu.VMEM((4, width), BF16),
             pltpu.VMEM((shard, width), F32),
             dma(()),
+            dma(()),
         ],
-    )(packed.reshape(all_blocks, BLOCK), features, projected, encoder_geometry)
+        compiler_params=pltpu.CompilerParams(vmem_limit_bytes=16 << 20),
+    )(packed.reshape(all_blocks, BLOCK), features, projected, hbm(encoder_geometry))
     far_rows = n_mesh * COARSE
     groups = far_rows // own_rows
     table_rows = shard + n_edge * far_rows
+    chips = n_edge // 2
+    chip_rows = chips * own_rows
     weights = [
         encoder_outer,
         node_first,
@@ -701,7 +855,7 @@
         update_state,
         update_outer,
     ]
-    return pl.pallas_call(
+    output, gradient = pl.pallas_call(
         functools.partial(process_kernel, n_mesh, n_edge),
         out_shape=(
             jax.ShapeDtypeStruct((own_rows, width), BF16),
@@ -712,28 +866,30 @@
         scratch_shapes=[pltpu.VMEM((width, width), BF16) for _ in weights]
         + [
             pltpu.VMEM((128, 128), F32),
-            pltpu.VMEM((8, edges), F32),
+            pltpu.VMEM((8, 2 * edges), F32),
             pltpu.VMEM((n_edge, own_rows, width), BF16),
             pltpu.VMEM((n_edge, own_rows, width), BF16),
             pltpu.VMEM((COARSE, width), BF16),
             pltpu.VMEM((n_mesh, COARSE, width), BF16),
             pltpu.VMEM((n_edge, groups, own_rows, width), BF16),
-            pltpu.VMEM((edges, table_rows), BF16),
-            pltpu.VMEM((edges, shard), BF16),
-            pltpu.VMEM((table_rows, edges), BF16),
-            pltpu.VMEM((shard, edges), BF16),
-            pltpu.VMEM((edges, width), F32),
-            pltpu.VMEM((edges, width), F32),
-            pltpu.VMEM((shard, width), BF16),
+            pltpu.VMEM((2 * edges, table_rows), BF16),
+            pltpu.VMEM((2 * edges, shard), BF16),
+            pltpu.VMEM((chip_rows + chips * far_rows, 2 * edges), BF16),
+            pltpu.VMEM((chip_rows, 2 * edges), BF16),
+            pltpu.VMEM((2 * edges, width), F32),
+            pltpu.VMEM((2 * edges, width), F32),
+            pltpu.VMEM((chip_rows, width), BF16),
+            pltpu.VMEM((chips, own_rows, width), BF16),
             pltpu.VMEM((n_edge, own_rows, width), BF16),
-            pltpu.VMEM((n_edge, own_rows, width), BF16),
-            pltpu.VMEM((shard, width), BF16),
-            pltpu.VMEM((n_edge, own_rows, width), BF16),
-            pltpu.VMEM((n_edge, far_rows, width), BF16),
-            pltpu.VMEM((n_edge, far_rows, width), BF16),
+            pltpu.VMEM((chip_rows, width), BF16),
+            pltpu.VMEM((chips, own_rows, width), BF16),
+            pltpu.VMEM((chips * far_rows, width), BF16),
+            pltpu.VMEM((chips, far_rows, width), BF16),
             pltpu.VMEM((n_mesh, COARSE, width), BF16),
             pltpu.VMEM((n_mesh, COARSE, width), BF16),
             pltpu.VMEM((own_rows, width), F32),
+            pltpu.VMEM((width, width), BF16),
+            pltpu.VMEM((width, width), BF16),
             dma((9,)),
             dma((6, n_edge)),
             dma((6, n_edge)),
@@ -741,21 +897,34 @@
             dma((n_mesh,)),
             dma((groups, n_edge)),
             dma((groups, n_edge)),
+            dma((groups, n_edge)),
             dma((n_mesh,)),
             dma((n_mesh,)),
         ],
-        compiler_params=pltpu.CompilerParams(collective_id=1, has_side_effects=True),
+        compiler_params=pltpu.CompilerParams(
+            collective_id=1, has_side_effects=True, vmem_limit_bytes=28 << 20
+        ),
     )(
         partial,
         mesh_position,
-        mesh_senders.reshape(1, edges),
-        mesh_receivers.reshape(1, edges),
-        mesh_features,
+        pair_senders,
+        pair_receivers,
+        pair_features,
         cotangent,
         node_position,
         edge_geometry,
-        *weights,
+        *[hbm(weight) for weight in weights],
     )
+    return pl.pallas_call(
+        finish_kernel,
+        out_shape=(
+            jax.ShapeDtypeStruct((own_rows, width), BF16),
+            jax.ShapeDtypeStruct((own_rows, width), F32),
+        ),
+        in_specs=[vmem()] * 2,
+        out_specs=(vmem(), vmem()),
+        compiler_params=pltpu.CompilerParams(vmem_limit_bytes=1 << 20),
+    )(output, gradient)
 
 
 def solution(mesh):

time: 98 us -> 85.7 us (0.87); the launches traced: 96.2 us -> 85.2 us
  Pallas kernels: 90.9 us -> 83.8 us
  local copies, waits for them, and re-layouts: 3.98 us -> 0.03 us
    unnamed x5 -> x8, local copies, waits for them, and re-layouts: 3.98 us -> 0.03 us
    pallas_call x1, Pallas kernels: 7.76 us -> 4.37 us  [shards(): pl.pallas_call(functools.partial(encode_kernel, n_edge, shard), out_shape...]
    pallas_call x1, Pallas kernels: 73.7 us -> 70.5 us  [shards(): pl.pallas_call(functools.partial(process_kernel, n_mesh, n_edge), out_sha...]
    pallas_call x1, Pallas kernels: 9.38 us -> 8.26 us  [shards(): pl.pallas_call(functools.partial(embed_kernel, n_edge), out_shape=(jax.Sh...]
where the time goes in v2:
time: 85.7 us; the launch traced here: 85.2 us
  Pallas kernels  83.8 us (98%)
  between operations  1.37 us (2%)
    pallas_call x1, Pallas kernels, shards(): pl.pallas_call(functools.partial(process_kernel, n_mesh, n_edge), out_sha...  70.5 us
    pallas_call x1, Pallas kernels, shards(): pl.pallas_call(functools.partial(embed_kernel, n_edge), out_shape=(jax.Sh...  8.26 us
    pallas_call x1, Pallas kernels, shards(): pl.pallas_call(functools.partial(encode_kernel, n_edge, shard), out_shape...  4.37 us

profile of v2, /device:TPU:40, one launch (start us, length us, event | category | flops | bytes accessed | tf_op | source)
XLA Modules:
  0.0 85.2 jit_solution(14521653980774322141)
XLA Ops:
  1.3 8.3 %shard_map.248 = (s32[8,16,128]{2,1,0:T(8,128)S(1)}, bf16[8,4,2048]{2,1,0:T(4,128)(2,1)S(1)}, bf16[512,512]{1,0:T(8,128)(2,1)S(1)}, s32[2,1,256]{2,1,0:T(1,128)S...) custom-call(s32[1]{0:T(128)S(6)} %copy.27.count, s32[16,128]{1,0:T(8,128)} %bitcast.8, s32[16,128]{1,0:T(8,128)} %bitcast.9, ...), custom_call_target="tpu_custom_call" | custom-call | tf_op jit(solution)/shard_map/pallas_call | solution.py:780
  9.5 0.0 copy-start
  9.6 0.0 copy-start.1
  9.6 0.0 copy-start.2
  9.6 0.0 copy-start.3
  9.6 4.4 %shard_map.249.partial = bf16[128,512]{1,0:T(8,128)(2,1)S(1)} custom-call(s32[128,128]{1,0:T(8,128)S(1)} %bitcast.6, bf16[8,4,2048]{2,1,0:T(4,128)(2,1)S(1)} %get-tuple-element.11.features, bf16[512,512]{1,0:T(8,128)(2,1)S(1)} %get-tuple-element.12.projected, bf16[4,512]{1,0:T(4,128)(2,1)} %geometry.2), custom_call_target="tpu_custom_call" | custom-call | tf_op jit(solution)/shard_map/pallas_call | solution.py:824
  14.0 0.0 copy-done
  14.0 0.0 copy-done.1
  14.0 0.0 copy-done.2
  14.0 0.0 copy-done.3
  14.0 70.5 %shard_map.250 = (bf16[16,512]{1,0:T(8,128)(2,1)S(1)}, f32[16,512]{1,0:T(8,128)S(1)}) custom-call(bf16[128,512]{1,0:T(8,128)(2,1)S(1)} %shard_map.249.partial, bf16[3,16]{1,0:T(4,128)(2,1)S(1)} %copy-done.3, s32[2,1,256]{2,1,0:T(1,128)S(1)} %get-tuple-element.13.pair_senders, s32[2,1,256]{2,1,0:T(1,128)S(1)} %get-tuple-element.14.pair_receivers, ...), custom_call_target="tpu_custom_call" | custom-call | tf_op jit(solution)/shard_map/pallas_call | solution.py:858
  84.5 0.6 shard_map.251
Async XLA Ops:
  9.5 4.4 %copy-start = (bf16[16,512]{1,0:T(8,128)(2,1)S(1)}, bf16[16,512]{1,0:T(8,128)(2,1)}, u32[]{:S(2)}) copy-start(bf16[16,512]{1,0:T(8,128)(2,1)} %cotangent.1) | copy-start | bytes 49156
  9.6 4.4 %copy-start.1 = (bf16[3,512]{1,0:T(4,128)(2,1)S(1)}, bf16[3,512]{1,0:T(4,128)(2,1)}, u32[]{:S(2)}) copy-start(bf16[3,512]{1,0:T(4,128)(2,1)} %node_position.1) | copy-start | bytes 9220
  9.6 4.4 %copy-start.2 = (bf16[4,512]{1,0:T(4,128)(2,1)S(1)}, bf16[4,512]{1,0:T(4,128)(2,1)}, u32[]{:S(2)}) copy-start(bf16[4,512]{1,0:T(4,128)(2,1)} %geometry.3) | copy-start | bytes 12292
  9.6 4.4 %copy-start.3 = (bf16[3,16]{1,0:T(4,128)(2,1)S(1)}, bf16[3,16]{1,0:T(4,128)(2,1)}, u32[]{:S(2)}) copy-start(bf16[3,16]{1,0:T(4,128)(2,1)} %mesh_position.1) | copy-start | bytes 292

commit v3 on v2

--- a/solution.py
+++ b/solution.py
@@ -249,6 +249,7 @@
     rank = nn(own_b, upper)
     per_block = nn(own_b, ones)
     base = nn(lower, per_block.astype(BF16))
+    aligned = base.astype(I32) & -BLOCK
     position[...] = jnp.where(own, (rank + base).astype(I32), -1)
     totals = nt(jnp.ones((8, BLOCK), BF16), own_b)
     starts = nn(totals.astype(BF16), before)
@@ -259,7 +260,6 @@
     queue[...] = jnp.zeros_like(queue)
     total[...] = jnp.zeros_like(total)
     geometry_v[...] = jnp.zeros_like(geometry_v)
-    copy.wait()
     chunk = CHUNK_ROWS * BLOCK
     per_chunk = per_device // CHUNK_ROWS
 
@@ -277,15 +277,22 @@
         parts = jnp.where(place == 6, ((code_row & (shard - 1)) + 1).astype(F32), parts)
         return parts.astype(BF16), where_row
 
-    def fill(parts, where_row, offset):
-        offset = pl.multiple_of(offset, BLOCK)
-        hits = one_hot(iota((WINDOW, chunk), 0) == where_row - offset)
-        queue[:, pl.ds(offset, WINDOW)] += nt(parts, hits)
-
+    def sorted_window(parts, where_row):
+        return nt(parts, one_hot(iota((WINDOW, chunk), 0) == where_row))
+
+    def add(offset, window):
+        queue[:, pl.ds(pl.multiple_of(offset, BLOCK), WINDOW)] += window
+
+    windows = []
     for device in range(n_edge):
         c = device * per_chunk
         parts, where_row = chunk_of(c, device, 0, c * CHUNK_ROWS)
-        fill(parts, where_row, bounds[0, c * CHUNK_ROWS] & -BLOCK)
+        from_row = aligned[c * CHUNK_ROWS : c * CHUNK_ROWS + 1, :]
+        from_row = jnp.concatenate([from_row] * CHUNK_ROWS, axis=1)
+        windows.append(sorted_window(parts, where_row - from_row))
+    copy.wait()
+    for device, window in enumerate(windows):
+        add(bounds[0, device * per_chunk * CHUNK_ROWS] & -BLOCK, window)
 
     def sort_chunk(c, carry):
         first = bounds[0, c * CHUNK_ROWS]
@@ -301,7 +308,8 @@
             parts, where_row = chunk_of(c, c >> bits(per_chunk), lane, row)
 
             def more(w, inner_carry):
-                fill(parts, where_row, start + w * WINDOW)
+                offset = start + w * WINDOW
+                add(offset, sorted_window(parts, where_row - offset))
                 return inner_carry
 
             lax.fori_loop(0, (last - start + WINDOW - 1) >> bits(WINDOW), more, 0)
@@ -407,6 +415,8 @@
     forward_send,
     final_send,
     final_recv,
+    band_ready,
+    far_ready,
 ):
     me = lax.axis_index("edge")
     band = lax.axis_index("mesh")
@@ -434,24 +444,44 @@
     ]
     for load in loads:
         load.start()
-    greet("edge", n_edge)
-    greet("mesh", n_mesh)
-
-    padded[...] = jnp.zeros_like(padded)
-    padded[0:3, 0:own_rows] = mesh_position[...].astype(F32)
-    place_columns = padded[...].T
-    position_term = jnp.zeros((own_rows, node_position.shape[1]), F32)
-    for k in range(3):
-        position_term += (
-            place_columns[0:own_rows, k : k + 1] * node_position[k : k + 1, :].astype(F32)
-        )
-
-    pl.semaphore_wait(pltpu.get_barrier_semaphore(), n_edge - 1 + n_mesh - 1)
-
     core = me & 1
     chip = me >> 1
     chips = n_edge // 2
     chip_rows = chips * own_rows
+    barrier = pltpu.get_barrier_semaphore()
+
+    def signal_band(k, carry):
+        @pl.when((k > 0) | (core == 1))
+        def _():
+            pl.semaphore_signal(
+                barrier,
+                inc=1,
+                device_id={"edge": 2 * ((chip + k) & (chips - 1))},
+                device_id_type=MESH,
+            )
+
+        return carry
+
+    def signal_far(k, carry):
+        pl.semaphore_signal(
+            barrier,
+            inc=1,
+            device_id={"mesh": (band + k) & (n_mesh - 1), "edge": me | 1},
+            device_id_type=MESH,
+        )
+        return carry
+
+    lax.fori_loop(0, chips, signal_band, 0)
+    lax.fori_loop(1, n_mesh, signal_far, 0)
+
+    @pl.when(core == 0)
+    def _():
+        pl.semaphore_wait(barrier, n_edge - 1)
+        pl.semaphore_signal(band_ready, inc=1, device_id={"edge": me ^ 1}, device_id_type=MESH)
+
+    @pl.when(core == 1)
+    def _():
+        pl.semaphore_wait(band_ready, 1)
 
     def each_chip(action):
         def step(k, carry):
@@ -515,6 +545,15 @@
     own_slice = pl.ds(pl.multiple_of(me * own_rows, own_rows), own_rows)
     start_all(0, rows_of(partial), enc_land)
     enc_land[me] = partial[own_slice, :]
+
+    padded[...] = jnp.zeros_like(padded)
+    padded[0:3, 0:own_rows] = mesh_position[...].astype(F32)
+    place_columns = padded[...].T
+    position_term = jnp.zeros((own_rows, node_position.shape[1]), F32)
+    for k in range(3):
+        position_term += (
+            place_columns[0:own_rows, k : k + 1] * node_position[k : k + 1, :].astype(F32)
+        )
 
     sender = jnp.concatenate([pair_senders[0], pair_senders[1]], axis=1)
     receiver = jnp.concatenate([pair_receivers[0], pair_receivers[1]], axis=1)
@@ -567,6 +606,9 @@
     coarse_own[...] = latent[0:COARSE, :]
     latents[me] = latent
 
+    latent_rows = lambda peer: latents.at[me]
+    start_all(1, latent_rows, latents)
+
     def far_copy(place, land):
         return pltpu.make_async_remote_copy(
             src_ref=coarse_own,
@@ -582,9 +624,16 @@
         far_copy(place, place_of(-step_of(place), n_mesh)).start()
         return carry
 
+    @pl.when(core == 1)
+    def _():
+        pl.semaphore_wait(barrier, 2 * (n_mesh - 1))
+        pl.semaphore_signal(far_ready, inc=1, device_id={"edge": me ^ 1}, device_id_type=MESH)
+
+    @pl.when(core == 0)
+    def _():
+        pl.semaphore_wait(far_ready, 1)
+
     lax.fori_loop(1, n_mesh, far_start, 0)
-    latent_rows = lambda peer: latents.at[me]
-    start_all(1, latent_rows, latents)
     coarse_land[0] = coarse_own[...]
 
     def relay(group, owner, peer):
@@ -900,6 +949,8 @@
             dma((groups, n_edge)),
             dma((n_mesh,)),
             dma((n_mesh,)),
+            pltpu.SemaphoreType.REGULAR,
+            pltpu.SemaphoreType.REGULAR,
         ],
         compiler_params=pltpu.CompilerParams(
             collective_id=1, has_side_effects=True, vmem_limit_bytes=28 << 20

time: 85.7 us -> 80.8 us (0.943)
  Pallas kernels: 83.8 us -> 79.2 us
    pallas_call x1, Pallas kernels: 70.5 us -> 66.5 us  [shards(): pl.pallas_call(functools.partial(process_kernel, n_mesh, n_edge), out_sha...]
where the time goes in v3:
time: 80.8 us; the launch traced here: 80.6 us
  Pallas kernels  79.2 us (98%)
  between operations  1.37 us (2%)
    pallas_call x1, Pallas kernels, shards(): pl.pallas_call(functools.partial(process_kernel, n_mesh, n_edge), out_sha...  66.5 us
    pallas_call x1, Pallas kernels, shards(): pl.pallas_call(functools.partial(embed_kernel, n_edge), out_shape=(jax.Sh...  8.26 us
    pallas_call x1, Pallas kernels, shards(): pl.pallas_call(functools.partial(encode_kernel, n_edge, shard), out_shape...  3.85 us

profile of v3, /device:TPU:40, one launch (start us, length us, event | category | flops | bytes accessed | tf_op | source)
XLA Modules:
  0.0 80.6 jit_solution(6313839956508431103)
XLA Ops:
  1.3 8.3 %shard_map.248 = (s32[8,16,128]{2,1,0:T(8,128)S(1)}, bf16[8,4,2048]{2,1,0:T(4,128)(2,1)S(1)}, bf16[512,512]{1,0:T(8,128)(2,1)S(1)}, s32[2,1,256]{2,1,0:T(1,128)S...) custom-call(s32[1]{0:T(128)S(6)} %copy.27.count, s32[16,128]{1,0:T(8,128)} %bitcast.8, s32[16,128]{1,0:T(8,128)} %bitcast.9, ...), custom_call_target="tpu_custom_call" | custom-call | tf_op jit(solution)/shard_map/pallas_call | solution.py:829
  9.5 0.0 copy-start
  9.6 0.0 copy-start.1
  9.6 0.0 copy-start.2
  9.6 0.0 copy-start.3
  9.6 3.8 %shard_map.249.partial = bf16[128,512]{1,0:T(8,128)(2,1)S(1)} custom-call(s32[128,128]{1,0:T(8,128)S(1)} %bitcast.6, bf16[8,4,2048]{2,1,0:T(4,128)(2,1)S(1)} %get-tuple-element.11.features, bf16[512,512]{1,0:T(8,128)(2,1)S(1)} %get-tuple-element.12.projected, bf16[4,512]{1,0:T(4,128)(2,1)} %geometry.2), custom_call_target="tpu_custom_call" | custom-call | tf_op jit(solution)/shard_map/pallas_call | solution.py:873
  13.4 0.0 copy-done
  13.5 0.0 copy-done.1
  13.5 0.0 copy-done.2
  13.5 0.0 copy-done.3
  13.5 66.5 %shard_map.250 = (bf16[16,512]{1,0:T(8,128)(2,1)S(1)}, f32[16,512]{1,0:T(8,128)S(1)}) custom-call(bf16[128,512]{1,0:T(8,128)(2,1)S(1)} %shard_map.249.partial, bf16[3,16]{1,0:T(4,128)(2,1)S(1)} %copy-done.3, s32[2,1,256]{2,1,0:T(1,128)S(1)} %get-tuple-element.13.pair_senders, s32[2,1,256]{2,1,0:T(1,128)S(1)} %get-tuple-element.14.pair_receivers, ...), custom_call_target="tpu_custom_call" | custom-call | tf_op jit(solution)/shard_map/pallas_call | solution.py:907
  80.0 0.6 shard_map.251
Async XLA Ops:
  9.5 3.9 %copy-start = (bf16[16,512]{1,0:T(8,128)(2,1)S(1)}, bf16[16,512]{1,0:T(8,128)(2,1)}, u32[]{:S(2)}) copy-start(bf16[16,512]{1,0:T(8,128)(2,1)} %cotangent.1) | copy-start | bytes 49156
  9.6 3.9 %copy-start.1 = (bf16[3,512]{1,0:T(4,128)(2,1)S(1)}, bf16[3,512]{1,0:T(4,128)(2,1)}, u32[]{:S(2)}) copy-start(bf16[3,512]{1,0:T(4,128)(2,1)} %node_position.1) | copy-start | bytes 9220
  9.6 3.9 %copy-start.2 = (bf16[4,512]{1,0:T(4,128)(2,1)S(1)}, bf16[4,512]{1,0:T(4,128)(2,1)}, u32[]{:S(2)}) copy-start(bf16[4,512]{1,0:T(4,128)(2,1)} %geometry.3) | copy-start | bytes 12292
  9.6 3.9 %copy-start.3 = (bf16[3,16]{1,0:T(4,128)(2,1)S(1)}, bf16[3,16]{1,0:T(4,128)(2,1)}, u32[]{:S(2)}) copy-start(bf16[3,16]{1,0:T(4,128)(2,1)} %mesh_position.1) | copy-start | bytes 292

commit v4 on v3

--- a/solution.py
+++ b/solution.py
@@ -69,14 +69,25 @@
     lax.fori_loop(1, count, signal, 0)
 
 
-def each_peer(axis, count, action):
-    me = lax.axis_index(axis)
-
-    def step(k, carry):
-        action(me, lax.rem(me + k, count))
-        return carry
-
-    lax.fori_loop(1, count, step, 0)
+def chip_steps(chips):
+    return sorted(range(1, chips), key=lambda step: -min(step, chips - step))
+
+
+def each_chip(n_edge, action):
+    me = lax.axis_index("edge")
+    chips = n_edge // 2
+    for step in chip_steps(chips):
+        action((me + 2 * step) & (n_edge - 1))
+
+
+def each_peer(n_edge, action):
+    me = lax.axis_index("edge")
+    chips = n_edge // 2
+    for step in chip_steps(chips):
+        peer = (me + 2 * step) & (n_edge - 1)
+        action(me, peer)
+        action(me, peer ^ 1)
+    action(me, me ^ 1)
 
 
 def embed_kernel(
@@ -172,7 +183,7 @@
         copy_packed(own, peer, peer).start()
         copy_features(own, peer, peer).start()
 
-    each_peer("edge", n_edge, send)
+    each_peer(n_edge, send)
 
     def copy_pair(ref, slot, k):
         return pltpu.make_async_remote_copy(
@@ -197,12 +208,15 @@
     projected[...] = tt(inner_v[...], latent).astype(BF16)
 
     def arrive(own, peer):
+        copy_packed(peer, peer, peer).wait_recv()
+        copy_features(peer, peer, peer).wait_recv()
+
+    def sent(own, peer):
         copy_packed(own, peer, peer).wait_send()
         copy_features(own, peer, peer).wait_send()
-        copy_packed(peer, peer, peer).wait_recv()
-        copy_features(peer, peer, peer).wait_recv()
-
-    each_peer("edge", n_edge, arrive)
+
+    each_peer(n_edge, arrive)
+    each_peer(n_edge, sent)
     for k, ref in enumerate(pairs):
         copy_pair(ref, core, k).wait_send()
         copy_pair(ref, core ^ 1, k).wait_recv()
@@ -483,12 +497,7 @@
     def _():
         pl.semaphore_wait(band_ready, 1)
 
-    def each_chip(action):
-        def step(k, carry):
-            action(((chip + k) & (chips - 1)) * 2 + core)
-            return carry
-
-        lax.fori_loop(1, chips, step, 0)
+    unsent = []
 
     def to_peer(phase, src, dst, sem, land):
         def copy(peer):
@@ -504,18 +513,18 @@
         return copy
 
     def start_all(phase, src, dst):
+        def start(own, peer):
+            copy = to_peer(phase, src, dst.at[own], lambda p: p, own)(peer)
+            copy.start()
+            unsent.append(copy)
+
+        each_peer(n_edge, start)
+
+    def wait_all(phase, src, dst):
         each_peer(
-            "edge",
             n_edge,
-            lambda own, peer: to_peer(phase, src, dst.at[own], lambda p: p, own)(peer).start(),
-        )
-
-    def wait_all(phase, src, dst):
-        def finish(own, peer):
-            to_peer(phase, src, dst.at[own], lambda p: p, own)(peer).wait_send()
-            to_peer(phase, src, dst.at[peer], lambda p: p, peer)(peer).wait_recv()
-
-        each_peer("edge", n_edge, finish)
+            lambda own, peer: to_peer(phase, src, dst.at[peer], lambda p: p, peer)(peer).wait_recv(),
+        )
 
     def chip_all(phase, ref, land, rows):
         def copy(peer, slot):
@@ -529,13 +538,17 @@
                 device_id_type=MESH,
             )
 
+        def begin(peer):
+            sent = copy(peer, chip)
+            sent.start()
+            unsent.append(sent)
+
         def start():
-            each_chip(lambda peer: copy(peer, chip).start())
+            each_chip(n_edge, begin)
             land[chip] = ref[pl.ds(pl.multiple_of(chip * rows, rows), rows), :]
 
         def finish():
-            each_chip(lambda peer: copy(peer, chip).wait_send())
-            each_chip(lambda peer: copy(peer, peer >> 1).wait_recv())
+            each_chip(n_edge, lambda peer: copy(peer, peer >> 1).wait_recv())
 
         return start, finish
 
@@ -563,7 +576,10 @@
     far_place = place_of(owner_band - band, n_mesh)
     far_row = far_place * COARSE + (sender & (COARSE - 1))
     local = sender - band * shard
-    pick = jnp.where(near, local, shard + owner_edge * far_rows + far_row)
+    place_low = far_place & (per_group - 1)
+    far_slot = ((far_place >> bits(per_group)) * n_edge + owner_edge) * own_rows
+    far_slot = far_slot + place_low * COARSE + (sender & (COARSE - 1))
+    pick = jnp.where(near, local, shard + far_slot)
     receiver = receiver - band * shard
     table_rows = shard + n_edge * far_rows
 
@@ -659,9 +675,31 @@
     def pass_on(group):
         def step(owner):
             relay(group, owner, owner).wait_recv()
-            forward(group, owner).start()
-
-        each_chip(step)
+            copy = forward(group, owner)
+            copy.start()
+            unsent.append(copy)
+
+        each_chip(n_edge, step)
+
+    def relay_start(group, peer):
+        copy = relay(group, me, peer)
+        copy.start()
+        unsent.append(copy)
+
+    def take_in(group):
+        each_chip(n_edge, lambda peer: forward(group, peer ^ 1).wait_recv())
+        relay(group, me ^ 1, me).wait_recv()
+        table = coarse[:, group].reshape(n_edge * own_rows, width)
+        table = nn(table, edge_sender[...]).astype(BF16)
+        first = shard + group * n_edge * own_rows
+        edge_term[...] += nn(send_pick[:, first : first + n_edge * own_rows], table)
+
+    edge_update[...] = nn(edge_outer[...], update_message[...]).astype(BF16)
+    wait_all(1, latent_rows, latents)
+    band_latent = latents[...].reshape(shard, width)
+    near_table = nn(band_latent, edge_sender[...]).astype(BF16)
+    recv_table = nn(band_latent, edge_receiver[...]).astype(BF16)
+    edge_term[...] += nn(send_pick[:, 0:shard], near_table) + nn(recv_pick[...], recv_table)
 
     for group in range(groups):
         for k in range(per_group):
@@ -670,38 +708,17 @@
                 far_copy(place, place).wait_recv()
         rows = [coarse_land[group * per_group + k].astype(F32) for k in range(per_group)]
         coarse[me, group] = jnp.concatenate(rows, axis=0).astype(BF16)
-        each_chip(lambda peer: relay(group, me, peer).start())
-        relay(group, me, me ^ 1).start()
+        each_chip(n_edge, lambda peer: relay_start(group, peer))
+        relay_start(group, me ^ 1)
         if group > 0:
             pass_on(group - 1)
+        if group > 1:
+            take_in(group - 2)
+    if groups > 1:
+        take_in(groups - 2)
     pass_on(groups - 1)
-
-    edge_update[...] = nn(edge_outer[...], update_message[...]).astype(BF16)
-    wait_all(1, latent_rows, latents)
-    band_latent = latents[...].reshape(shard, width)
-    recv_rows = nn(recv_pick[...], band_latent).astype(BF16)
-    send_rows = nn(send_pick[:, 0:shard], band_latent)
-    edge_term[...] += nn(recv_rows, edge_receiver[...])
-
-    def far_finish(k, carry):
-        far_copy(k, k).wait_send()
-        return carry
-
-    lax.fori_loop(1, n_mesh, far_finish, 0)
-    for group in range(groups):
-
-        def relay_finish(peer):
-            relay(group, me, peer).wait_send()
-            forward(group, peer).wait_send()
-            forward(group, peer ^ 1).wait_recv()
-
-        each_chip(relay_finish)
-        relay(group, me, me ^ 1).wait_send()
-        relay(group, me ^ 1, me).wait_recv()
-
-    far_latent = coarse[...].reshape(n_edge * far_rows, width)
-    send_rows = (send_rows + nn(send_pick[:, shard:], far_latent)).astype(BF16)
-    pre = edge_term[...] + nn(send_rows, edge_sender[...])
+    take_in(groups - 1)
+    pre = edge_term[...]
     sigma = sigmoid(pre)
     act = (pre * sigma).astype(BF16)
     slope[...] = sigma * (1.0 + pre * (1.0 - sigma))
@@ -759,7 +776,6 @@
     result = grad_node + jnp.sum(back_band_land[...].astype(F32), axis=0)
 
     def final_finish(k, carry):
-        final_copy(k, k).wait_send()
         final_copy(k, k).wait_recv()
         return carry
 
@@ -770,6 +786,15 @@
     tail[...] = jnp.zeros_like(tail)
     tail[0:COARSE, :] = arrived
     gradient[...] = result + nt(tail[...].astype(BF16), edge_sender[...])
+
+    def far_sent(k, carry):
+        far_copy(k, k).wait_send()
+        final_copy(k, k).wait_send()
+        return carry
+
+    lax.fori_loop(1, n_mesh, far_sent, 0)
+    for copy in unsent:
+        copy.wait_send()
 
 
 def finish_kernel(output, gradient, output_copy, gradient_copy):

time: 80.8 us -> 80.5 us (level)
  no operation moved by 1% of the time
where the time goes in v4:
time: 80.5 us; the launch traced here: 80.3 us
  Pallas kernels  78.9 us (98%)
  between operations  1.37 us (2%)
    pallas_call x1, Pallas kernels, shards(): pl.pallas_call(functools.partial(process_kernel, n_mesh, n_edge), out_sha...  66.7 us
    pallas_call x1, Pallas kernels, shards(): pl.pallas_call(functools.partial(embed_kernel, n_edge), out_shape=(jax.Sh...  7.73 us
    pallas_call x1, Pallas kernels, shards(): pl.pallas_call(functools.partial(encode_kernel, n_edge, shard), out_shape...  3.9 us

profile of v4, /device:TPU:40, one launch (start us, length us, event | category | flops | bytes accessed | tf_op | source)
XLA Modules:
  0.0 80.3 jit_solution(16265085150360162476)
XLA Ops:
  1.3 7.7 %shard_map.248 = (s32[8,16,128]{2,1,0:T(8,128)S(1)}, bf16[8,4,2048]{2,1,0:T(4,128)(2,1)S(1)}, bf16[512,512]{1,0:T(8,128)(2,1)S(1)}, s32[2,1,256]{2,1,0:T(1,128)S...) custom-call(s32[1]{0:T(128)S(6)} %copy.27.count, s32[16,128]{1,0:T(8,128)} %bitcast.8, s32[16,128]{1,0:T(8,128)} %bitcast.9, ...), custom_call_target="tpu_custom_call" | custom-call | tf_op jit(solution)/shard_map/pallas_call | solution.py:854
  9.0 0.0 copy-start
  9.0 0.0 copy-start.1
  9.0 0.0 copy-start.2
  9.1 0.0 copy-start.3
  9.1 3.9 %shard_map.249.partial = bf16[128,512]{1,0:T(8,128)(2,1)S(1)} custom-call(s32[128,128]{1,0:T(8,128)S(1)} %bitcast.6, bf16[8,4,2048]{2,1,0:T(4,128)(2,1)S(1)} %get-tuple-element.11.features, bf16[512,512]{1,0:T(8,128)(2,1)S(1)} %get-tuple-element.12.projected, bf16[4,512]{1,0:T(4,128)(2,1)} %geometry.2), custom_call_target="tpu_custom_call" | custom-call | tf_op jit(solution)/shard_map/pallas_call | solution.py:898
  13.0 0.0 copy-done
  13.0 0.0 copy-done.1
  13.0 0.0 copy-done.2
  13.0 0.0 copy-done.3
  13.0 66.7 %shard_map.250 = (bf16[16,512]{1,0:T(8,128)(2,1)S(1)}, f32[16,512]{1,0:T(8,128)S(1)}) custom-call(bf16[128,512]{1,0:T(8,128)(2,1)S(1)} %shard_map.249.partial, bf16[3,16]{1,0:T(4,128)(2,1)S(1)} %copy-done.3, s32[2,1,256]{2,1,0:T(1,128)S(1)} %get-tuple-element.13.pair_senders, s32[2,1,256]{2,1,0:T(1,128)S(1)} %get-tuple-element.14.pair_receivers, ...), custom_call_target="tpu_custom_call" | custom-call | tf_op jit(solution)/shard_map/pallas_call | solution.py:932
  79.7 0.6 shard_map.251
Async XLA Ops:
  9.0 4.0 %copy-start = (bf16[16,512]{1,0:T(8,128)(2,1)S(1)}, bf16[16,512]{1,0:T(8,128)(2,1)}, u32[]{:S(2)}) copy-start(bf16[16,512]{1,0:T(8,128)(2,1)} %cotangent.1) | copy-start | bytes 49156
  9.0 4.0 %copy-start.1 = (bf16[3,512]{1,0:T(4,128)(2,1)S(1)}, bf16[3,512]{1,0:T(4,128)(2,1)}, u32[]{:S(2)}) copy-start(bf16[3,512]{1,0:T(4,128)(2,1)} %node_position.1) | copy-start | bytes 9220
  9.0 4.0 %copy-start.2 = (bf16[4,512]{1,0:T(4,128)(2,1)S(1)}, bf16[4,512]{1,0:T(4,128)(2,1)}, u32[]{:S(2)}) copy-start(bf16[4,512]{1,0:T(4,128)(2,1)} %geometry.3) | copy-start | bytes 12292
  9.1 4.0 %copy-start.3 = (bf16[3,16]{1,0:T(4,128)(2,1)S(1)}, bf16[3,16]{1,0:T(4,128)(2,1)}, u32[]{:S(2)}) copy-start(bf16[3,16]{1,0:T(4,128)(2,1)} %mesh_position.1) | copy-start | bytes 292

commit v5 on v4

--- a/solution.py
+++ b/solution.py
@@ -106,9 +106,9 @@
     packed_all,
     features_all,
     projected,
-    pair_senders,
-    pair_receivers,
-    pair_features,
+    band_senders,
+    band_receivers,
+    band_features,
     senders_v,
     receivers_v,
     rows_v,
@@ -116,16 +116,11 @@
     second_v,
     inner_v,
     load_sem,
-    send_a,
-    send_b,
-    recv_a,
-    recv_b,
-    pair_send,
-    pair_recv,
+    send_sem,
+    recv_sem,
 ):
     me = lax.axis_index("edge")
     band = lax.axis_index("mesh")
-    core = me & 1
     loads = [
         pltpu.make_async_copy(src, dst, load_sem.at[k])
         for k, (src, dst) in enumerate(
@@ -133,9 +128,9 @@
                 (senders, senders_v),
                 (receivers, receivers_v),
                 (features, features_all.at[me]),
-                (mesh_senders, pair_senders.at[core]),
-                (mesh_receivers, pair_receivers.at[core]),
-                (mesh_features, pair_features.at[core]),
+                (mesh_senders, band_senders.at[me]),
+                (mesh_receivers, band_receivers.at[me]),
+                (mesh_features, band_features.at[me]),
                 (grid_input, rows_v),
                 (first, first_v),
                 (second, second_v),
@@ -159,45 +154,20 @@
         load.wait()
     pl.semaphore_wait(pltpu.get_barrier_semaphore(), n_edge - 1)
 
-    def copy_packed(owner, peer, sem):
+    tables = (packed_all, features_all, band_senders, band_receivers, band_features)
+
+    def copy(k, owner, peer):
         return pltpu.make_async_remote_copy(
-            src_ref=packed_all.at[owner],
-            dst_ref=packed_all.at[owner],
-            send_sem=send_a.at[sem],
-            recv_sem=recv_a.at[owner],
+            src_ref=tables[k].at[owner],
+            dst_ref=tables[k].at[owner],
+            send_sem=send_sem.at[k, peer],
+            recv_sem=recv_sem.at[k, owner],
             device_id={"edge": peer},
             device_id_type=MESH,
         )
 
-    def copy_features(owner, peer, sem):
-        return pltpu.make_async_remote_copy(
-            src_ref=features_all.at[owner],
-            dst_ref=features_all.at[owner],
-            send_sem=send_b.at[sem],
-            recv_sem=recv_b.at[owner],
-            device_id={"edge": peer},
-            device_id_type=MESH,
-        )
-
-    def send(own, peer):
-        copy_packed(own, peer, peer).start()
-        copy_features(own, peer, peer).start()
-
-    each_peer(n_edge, send)
-
-    def copy_pair(ref, slot, k):
-        return pltpu.make_async_remote_copy(
-            src_ref=ref.at[slot],
-            dst_ref=ref.at[slot],
-            send_sem=pair_send.at[k],
-            recv_sem=pair_recv.at[k],
-            device_id={"edge": me ^ 1},
-            device_id_type=MESH,
-        )
-
-    pairs = (pair_senders, pair_receivers, pair_features)
-    for k, ref in enumerate(pairs):
-        copy_pair(ref, core, k).start()
+    for group in ((0, 1), (2, 3, 4)):
+        each_peer(n_edge, lambda own, peer: [copy(k, own, peer).start() for k in group])
     loads[6].wait()
     loads[7].wait()
     hidden = tn(rows_v[...], first_v[...])
@@ -208,18 +178,15 @@
     projected[...] = tt(inner_v[...], latent).astype(BF16)
 
     def arrive(own, peer):
-        copy_packed(peer, peer, peer).wait_recv()
-        copy_features(peer, peer, peer).wait_recv()
+        for k in range(len(tables)):
+            copy(k, peer, peer).wait_recv()
 
     def sent(own, peer):
-        copy_packed(own, peer, peer).wait_send()
-        copy_features(own, peer, peer).wait_send()
+        for k in range(len(tables)):
+            copy(k, own, peer).wait_send()
 
     each_peer(n_edge, arrive)
     each_peer(n_edge, sent)
-    for k, ref in enumerate(pairs):
-        copy_pair(ref, core, k).wait_send()
-        copy_pair(ref, core ^ 1, k).wait_recv()
 
 
 def packed_shard(n_edge):
@@ -368,9 +335,9 @@
     n_edge,
     partial,
     mesh_position,
-    pair_senders,
-    pair_receivers,
-    pair_features,
+    band_senders,
+    band_receivers,
+    band_features,
     cotangent,
     node_position,
     geometry,
@@ -403,17 +370,15 @@
     coarse,
     send_pick,
     recv_pick,
-    send_drop,
     recv_drop,
+    back_drop,
     edge_term,
     slope,
-    proc_send,
-    proc_land,
-    grads,
-    back_band,
-    back_band_land,
-    back_coarse,
-    back_coarse_land,
+    cotangents,
+    state_term,
+    back_out,
+    update_act,
+    grad_pre,
     back_far,
     back_far_land,
     tail,
@@ -438,7 +403,8 @@
     shard = own_rows * n_edge
     groups = n_mesh * COARSE // own_rows
     per_group = own_rows // COARSE
-    edges = 2 * pair_senders.shape[2]
+    half = band_senders.shape[2]
+    edges = 2 * half
     far_rows = n_mesh * COARSE
     loads = [
         pltpu.make_async_copy(src, dst, load_sem.at[k])
@@ -461,7 +427,6 @@
     core = me & 1
     chip = me >> 1
     chips = n_edge // 2
-    chip_rows = chips * own_rows
     barrier = pltpu.get_barrier_semaphore()
 
     def signal_band(k, carry):
@@ -526,32 +491,6 @@
             lambda own, peer: to_peer(phase, src, dst.at[peer], lambda p: p, peer)(peer).wait_recv(),
         )
 
-    def chip_all(phase, ref, land, rows):
-        def copy(peer, slot):
-            start = pl.multiple_of((peer >> 1) * rows, rows)
-            return pltpu.make_async_remote_copy(
-                src_ref=ref.at[pl.ds(start, rows), :],
-                dst_ref=land.at[slot],
-                send_sem=send_sem.at[phase, peer],
-                recv_sem=recv_sem.at[phase, slot],
-                device_id={"edge": peer},
-                device_id_type=MESH,
-            )
-
-        def begin(peer):
-            sent = copy(peer, chip)
-            sent.start()
-            unsent.append(sent)
-
-        def start():
-            each_chip(n_edge, begin)
-            land[chip] = ref[pl.ds(pl.multiple_of(chip * rows, rows), rows), :]
-
-        def finish():
-            each_chip(n_edge, lambda peer: copy(peer, peer >> 1).wait_recv())
-
-        return start, finish
-
     def rows_of(ref):
         return lambda peer: ref.at[pl.ds(pl.multiple_of(peer * own_rows, own_rows), own_rows), :]
 
@@ -568,50 +507,55 @@
             place_columns[0:own_rows, k : k + 1] * node_position[k : k + 1, :].astype(F32)
         )
 
-    sender = jnp.concatenate([pair_senders[0], pair_senders[1]], axis=1)
-    receiver = jnp.concatenate([pair_receivers[0], pair_receivers[1]], axis=1)
-    owner_band = sender >> bits(shard)
-    near = owner_band == band
-    owner_edge = (sender >> bits(own_rows)) & (n_edge - 1)
-    far_place = place_of(owner_band - band, n_mesh)
-    far_row = far_place * COARSE + (sender & (COARSE - 1))
-    local = sender - band * shard
-    place_low = far_place & (per_group - 1)
-    far_slot = ((far_place >> bits(per_group)) * n_edge + owner_edge) * own_rows
-    far_slot = far_slot + place_low * COARSE + (sender & (COARSE - 1))
-    pick = jnp.where(near, local, shard + far_slot)
-    receiver = receiver - band * shard
-    table_rows = shard + n_edge * far_rows
-
-    def chip_row(row, owner):
-        own_core = (owner & 1) == core
-        return jnp.where(own_core, (owner >> 1) * own_rows + (row & (own_rows - 1)), -1)
-
-    drop_near = jnp.where(near, chip_row(local, owner_edge), -1)
-    drop_far = jnp.where((owner_edge & 1) == core, (owner_edge >> 1) * far_rows + far_row, -1)
-    drop_far = jnp.where(near, -1, drop_far)
-    drop_recv = chip_row(receiver, receiver >> bits(own_rows))
-    send_drop[0:chip_rows, :] = one_hot(iota((chip_rows, edges), 0) == drop_near)
-    send_drop[chip_rows:, :] = one_hot(iota((chips * far_rows, edges), 0) == drop_far)
-    recv_drop[...] = one_hot(iota((chip_rows, edges), 0) == drop_recv)
-    pick_columns = jnp.broadcast_to(pick.astype(F32), (128, edges)).T.astype(I32)
-    recv_columns = jnp.broadcast_to(receiver.astype(F32), (128, edges)).T.astype(I32)
-    lanes = iota((edges, 128), 1)
-    for k in range(table_rows // 128):
-        send_pick[:, k * 128 : (k + 1) * 128] = one_hot(lanes + k * 128 == pick_columns)
-    for k in range(shard // 128):
-        recv_pick[:, k * 128 : (k + 1) * 128] = one_hot(lanes + k * 128 == recv_columns)
-    small[...] = jnp.zeros_like(small)
-    half = edges // 2
-    small[0:4, 0:half] = pair_features[0].astype(F32)
-    small[0:4, half:edges] = pair_features[1].astype(F32)
     width = geometry.shape[1]
     padded_geometry = jnp.concatenate([geometry[...].astype(F32)] * 2, axis=0)
-    padded_geometry = jnp.where(iota((8, width), 0) < 4, padded_geometry, 0.0)
-    edge_term[...] = tn(small[...].astype(BF16), padded_geometry.astype(BF16))
+    padded_geometry = jnp.where(iota((8, width), 0) < 4, padded_geometry, 0.0).astype(BF16)
+    small[...] = jnp.zeros_like(small)
+    blocks = n_edge // 2
+    table_rows = shard + n_edge * far_rows
+
+    def block_rows(block):
+        return pl.ds(pl.multiple_of(block * edges, edges), edges)
+
+    def prepare(block, carry):
+        span = block_rows(block)
+        first, second = 2 * block, 2 * block + 1
+        sender = jnp.concatenate([band_senders[first], band_senders[second]], axis=1)
+        receiver = jnp.concatenate([band_receivers[first], band_receivers[second]], axis=1)
+        owner_band = sender >> bits(shard)
+        near = owner_band == band
+        owner_edge = (sender >> bits(own_rows)) & (n_edge - 1)
+        far_place = place_of(owner_band - band, n_mesh)
+        coarse_row = sender & (COARSE - 1)
+        far_slot = ((far_place >> bits(per_group)) * n_edge + owner_edge) * own_rows
+        far_slot = far_slot + (far_place & (per_group - 1)) * COARSE + coarse_row
+        local = sender - band * shard
+        receiver = receiver - band * shard
+        pick = jnp.where(near, local, shard + far_slot)
+        mine = owner_edge == me
+        drop_far = jnp.where(mine & (owner_band != band), far_place * COARSE + coarse_row, -1)
+        drop_near = jnp.where(mine & near, local & (own_rows - 1), -1)
+        drop_recv = jnp.where(receiver >> bits(own_rows) == me, receiver & (own_rows - 1), -1)
+        back_drop[0:far_rows, span] = one_hot(iota((far_rows, edges), 0) == drop_far)
+        base = far_rows + own_rows
+        back_drop[far_rows:base, span] = one_hot(iota((own_rows, edges), 0) == drop_near)
+        back_drop[base:, span] = one_hot(iota((own_rows, edges), 0) == drop_recv)
+        recv_drop[:, span] = one_hot(iota((shard, edges), 0) == receiver)
+        pick_columns = jnp.broadcast_to(pick.astype(F32), (128, edges)).T.astype(I32)
+        recv_columns = jnp.broadcast_to(receiver.astype(F32), (128, edges)).T.astype(I32)
+        lanes = iota((edges, 128), 1)
+        for k in range(table_rows // 128):
+            send_pick[span, k * 128 : (k + 1) * 128] = one_hot(lanes + k * 128 == pick_columns)
+        for k in range(shard // 128):
+            recv_pick[span, k * 128 : (k + 1) * 128] = one_hot(lanes + k * 128 == recv_columns)
+        small[0:4, 0:half] = band_features[first].astype(F32)
+        small[0:4, half:edges] = band_features[second].astype(F32)
+        edge_term[span, :] = tn(small[...].astype(BF16), padded_geometry)
+        return carry
+
+    lax.fori_loop(0, blocks, prepare, 0)
     for load in loads:
         load.wait()
-    back_out = nt(cotangent[...], update_outer[...])
     enc_node[...] = nn(encoder_outer[...], node_first[...]).astype(BF16)
 
     wait_all(0, rows_of(partial), enc_land)
@@ -624,6 +568,8 @@
 
     latent_rows = lambda peer: latents.at[me]
     start_all(1, latent_rows, latents)
+    start_all(2, lambda peer: cotangent, cotangents)
+    cotangents[me] = cotangent[...]
 
     def far_copy(place, land):
         return pltpu.make_async_remote_copy(
@@ -691,15 +637,35 @@
         relay(group, me ^ 1, me).wait_recv()
         table = coarse[:, group].reshape(n_edge * own_rows, width)
         table = nn(table, edge_sender[...]).astype(BF16)
-        first = shard + group * n_edge * own_rows
-        edge_term[...] += nn(send_pick[:, first : first + n_edge * own_rows], table)
+        return pl.ds(shard + group * n_edge * own_rows, n_edge * own_rows), table
+
+    def add_in(group):
+        columns, table = take_in(group)
+
+        def add(block, carry):
+            span = block_rows(block)
+            edge_term[span, :] += nn(send_pick[span, columns], table)
+            return carry
+
+        lax.fori_loop(0, blocks, add, 0)
 
     edge_update[...] = nn(edge_outer[...], update_message[...]).astype(BF16)
     wait_all(1, latent_rows, latents)
     band_latent = latents[...].reshape(shard, width)
     near_table = nn(band_latent, edge_sender[...]).astype(BF16)
     recv_table = nn(band_latent, edge_receiver[...]).astype(BF16)
-    edge_term[...] += nn(send_pick[:, 0:shard], near_table) + nn(recv_pick[...], recv_table)
+
+    def add_near(block, carry):
+        span = block_rows(block)
+        edge_term[span, :] += nn(send_pick[span, 0:shard], near_table) + nn(
+            recv_pick[span, :], recv_table
+        )
+        return carry
+
+    lax.fori_loop(0, blocks, add_near, 0)
+    state_term[...] = nn(band_latent, update_state[...])
+    wait_all(2, lambda peer: cotangent, cotangents)
+    back_out[...] = nt(cotangents[...].reshape(shard, width), update_outer[...])
 
     for group in range(groups):
         for k in range(per_group):
@@ -713,45 +679,31 @@
         if group > 0:
             pass_on(group - 1)
         if group > 1:
-            take_in(group - 2)
+            add_in(group - 2)
     if groups > 1:
-        take_in(groups - 2)
+        add_in(groups - 2)
     pass_on(groups - 1)
-    take_in(groups - 1)
-    pre = edge_term[...]
-    sigma = sigmoid(pre)
-    act = (pre * sigma).astype(BF16)
-    slope[...] = sigma * (1.0 + pre * (1.0 - sigma))
-    proc_send[...] = nn(recv_drop[...], act).astype(BF16)
-    proc_start, proc_finish = chip_all(2, proc_send, proc_land, own_rows)
-    proc_start()
-    state_term = nn(latents[me], update_state[...])
-    proc_finish()
-    proc_sum = jnp.sum(proc_land[...].astype(F32), axis=0)
-    update_pre = nn(proc_sum.astype(BF16), edge_update[...]) + state_term
+    columns, table = take_in(groups - 1)
+    proc_sum = jnp.zeros((shard, width), F32)
+    for block in range(blocks):
+        span = pl.ds(block * edges, edges)
+        pre = edge_term[span, :] + nn(send_pick[span, columns], table)
+        sigma = sigmoid(pre)
+        slope[span, :] = sigma * (1.0 + pre * (1.0 - sigma))
+        proc_sum = proc_sum + nn(recv_drop[:, span], (pre * sigma).astype(BF16))
+    update_pre = nn(proc_sum.astype(BF16), edge_update[...]) + state_term[...]
     sigma = sigmoid(update_pre)
-    grad_pre = (back_out * (sigma * (1.0 + update_pre * (1.0 - sigma)))).astype(BF16)
-    grads[me] = nt(grad_pre, edge_update[...]).astype(BF16)
-    grad_rows = lambda peer: grads.at[me]
-    start_all(3, grad_rows, grads)
-    update_act = (update_pre * sigma).astype(BF16)
-    mixed = latents[me].astype(F32) + nn(update_act, update_outer[...])
-    output[...] = mixed.astype(BF16)
-    grad_node = cotangent[...].astype(F32) + nt(grad_pre, update_state[...])
-    wait_all(3, grad_rows, grads)
-    band_grads = grads[...].reshape(shard, width)
-    grad_edge = (nn(recv_pick[...], band_grads) * slope[...]).astype(BF16)
-    back_coarse[...] = nn(send_drop[chip_rows:, :], grad_edge).astype(BF16)
-    coarse_start, coarse_finish = chip_all(4, back_coarse, back_coarse_land, far_rows)
-    coarse_start()
-    to_sender = nn(send_drop[0:chip_rows, :], grad_edge).astype(BF16)
-    to_receiver = nn(recv_drop[...], grad_edge).astype(BF16)
-    back = nt(to_sender, edge_sender[...]) + nt(to_receiver, edge_receiver[...])
-    back_band[...] = back.astype(BF16)
-    band_start, band_finish = chip_all(5, back_band, back_band_land, own_rows)
-    band_start()
-    coarse_finish()
-    far_total = jnp.sum(back_coarse_land[...].astype(F32), axis=0)
+    slopes = sigma * (1.0 + update_pre * (1.0 - sigma))
+    grad_all = (back_out[...] * slopes).astype(BF16)
+    grad_pre[...] = grad_all
+    update_act[...] = (update_pre * sigma).astype(BF16)
+    band_grads = nt(grad_all, edge_update[...]).astype(BF16)
+    back = jnp.zeros((far_rows + 2 * own_rows, width), F32)
+    for block in range(blocks):
+        span = pl.ds(block * edges, edges)
+        grad_edge = (nn(recv_pick[span, :], band_grads) * slope[span, :]).astype(BF16)
+        back = back + nn(back_drop[:, span], grad_edge)
+    far_total = back[0:far_rows, :]
 
     def final_copy(place, land):
         return pltpu.make_async_remote_copy(
@@ -772,8 +724,12 @@
         return carry
 
     lax.fori_loop(1, n_mesh, final_start, 0)
-    band_finish()
-    result = grad_node + jnp.sum(back_band_land[...].astype(F32), axis=0)
+    mixed = latents[me].astype(F32) + nn(update_act[own_slice, :], update_outer[...])
+    output[...] = mixed.astype(BF16)
+    grad_node = cotangent[...].astype(F32) + nt(grad_pre[own_slice, :], update_state[...])
+    to_receiver = back[far_rows + own_rows :, :].astype(BF16)
+    result = grad_node + nt(to_receiver, edge_receiver[...])
+    tail[...] = back[far_rows : far_rows + own_rows, :]
 
     def final_finish(k, carry):
         final_copy(k, k).wait_recv()
@@ -783,8 +739,7 @@
     arrived = back_far_land[1].astype(F32)
     for place in range(2, n_mesh):
         arrived = arrived + back_far_land[place].astype(F32)
-    tail[...] = jnp.zeros_like(tail)
-    tail[0:COARSE, :] = arrived
+    tail[0:COARSE, :] += arrived
     gradient[...] = result + nt(tail[...].astype(BF16), edge_sender[...])
 
     def far_sent(k, carry):
@@ -851,15 +806,15 @@
     shard = own_rows * n_edge
     edges = mesh_senders.shape[0]
     dma = pltpu.SemaphoreType.DMA
-    packed, features, projected, pair_senders, pair_receivers, pair_features = pl.pallas_call(
+    packed, features, projected, band_senders, band_receivers, band_features = pl.pallas_call(
         functools.partial(embed_kernel, n_edge),
         out_shape=(
             jax.ShapeDtypeStruct((n_edge, blocks, BLOCK), I32),
             jax.ShapeDtypeStruct((n_edge, 4, slots), BF16),
             jax.ShapeDtypeStruct((width, grid_rows), BF16),
-            jax.ShapeDtypeStruct((2, 1, edges), I32),
-            jax.ShapeDtypeStruct((2, 1, edges), I32),
-            jax.ShapeDtypeStruct((2, 4, edges), BF16),
+            jax.ShapeDtypeStruct((n_edge, 1, edges), I32),
+            jax.ShapeDtypeStruct((n_edge, 1, edges), I32),
+            jax.ShapeDtypeStruct((n_edge, 4, edges), BF16),
         ),
         in_specs=[pl.BlockSpec(memory_space=pltpu.SMEM)] + [anywhere()] * 10,
         out_specs=(vmem(),) * 6,
@@ -871,12 +826,8 @@
             pltpu.VMEM((width, width), BF16),
             pltpu.VMEM((width, width), BF16),
             dma((10,)),
-            dma((n_edge,)),
-            dma((n_edge,)),
-            dma((n_edge,)),
-            dma((n_edge,)),
-            dma((3,)),
-            dma((3,)),
+            dma((5, n_edge)),
+            dma((5, n_edge)),
         ],
         compiler_params=pltpu.CompilerParams(
             collective_id=0, has_side_effects=True, vmem_limit_bytes=12 << 20
@@ -916,8 +867,6 @@
     far_rows = n_mesh * COARSE
     groups = far_rows // own_rows
     table_rows = shard + n_edge * far_rows
-    chips = n_edge // 2
-    chip_rows = chips * own_rows
     weights = [
         encoder_outer,
         node_first,
@@ -946,27 +895,25 @@
             pltpu.VMEM((COARSE, width), BF16),
             pltpu.VMEM((n_mesh, COARSE, width), BF16),
             pltpu.VMEM((n_edge, groups, own_rows, width), BF16),
-            pltpu.VMEM((2 * edges, table_rows), BF16),
-            pltpu.VMEM((2 * edges, shard), BF16),
-            pltpu.VMEM((chip_rows + chips * far_rows, 2 * edges), BF16),
-            pltpu.VMEM((chip_rows, 2 * edges), BF16),
-            pltpu.VMEM((2 * edges, width), F32),
-            pltpu.VMEM((2 * edges, width), F32),
-            pltpu.VMEM((chip_rows, width), BF16),
-            pltpu.VMEM((chips, own_rows, width), BF16),
+            pltpu.VMEM((n_edge * edges, table_rows), BF16),
+            pltpu.VMEM((n_edge * edges, shard), BF16),
+            pltpu.VMEM((shard, n_edge * edges), BF16),
+            pltpu.VMEM((far_rows + 2 * own_rows, n_edge * edges), BF16),
+            pltpu.VMEM((n_edge * edges, width), F32),
+            pltpu.VMEM((n_edge * edges, width), F32),
             pltpu.VMEM((n_edge, own_rows, width), BF16),
-            pltpu.VMEM((chip_rows, width), BF16),
-            pltpu.VMEM((chips, own_rows, width), BF16),
-            pltpu.VMEM((chips * far_rows, width), BF16),
-            pltpu.VMEM((chips, far_rows, width), BF16),
+            pltpu.VMEM((shard, width), F32),
+            pltpu.VMEM((shard, width), F32),
+            pltpu.VMEM((shard, width), BF16),
+            pltpu.VMEM((shard, width), BF16),
             pltpu.VMEM((n_mesh, COARSE, width), BF16),
             pltpu.VMEM((n_mesh, COARSE, width), BF16),
             pltpu.VMEM((own_rows, width), F32),
             pltpu.VMEM((width, width), BF16),
             pltpu.VMEM((width, width), BF16),
             dma((9,)),
-            dma((6, n_edge)),
-            dma((6, n_edge)),
+            dma((3, n_edge)),
+            dma((3, n_edge)),
             dma((n_mesh,)),
             dma((n_mesh,)),
             dma((groups, n_edge)),
@@ -978,14 +925,14 @@
             pltpu.SemaphoreType.REGULAR,
         ],
         compiler_params=pltpu.CompilerParams(
-            collective_id=1, has_side_effects=True, vmem_limit_bytes=28 << 20
+            collective_id=1, has_side_effects=True, vmem_limit_bytes=36 << 20
         ),
     )(
         partial,
         mesh_position,
-        pair_senders,
-        pair_receivers,
-        pair_features,
+        band_senders,
+        band_receivers,
+        band_features,
         cotangent,
         node_position,
         edge_geometry,

time: 80.5 us -> 72.3 us (0.90); the launches traced: 80.3 us -> 71.1 us
  Pallas kernels: 78.9 us -> 69.7 us
    pallas_call x1, Pallas kernels: 66.7 us -> 55.9 us  [shards(): pl.pallas_call(functools.partial(process_kernel, n_mesh, n_edge), out_sha...]
    pallas_call x1, Pallas kernels: 7.73 us -> 9.21 us  [shards(): pl.pallas_call(functools.partial(embed_kernel, n_edge), out_shape=(jax.Sh...]
where the time goes in v5:
time: 72.3 us; the launch traced here: 71.1 us
  Pallas kernels  69.7 us (96%)
  between operations  1.37 us (2%)
    pallas_call x1, Pallas kernels, shards(): pl.pallas_call(functools.partial(process_kernel, n_mesh, n_edge), out_sha...  55.9 us
    pallas_call x1, Pallas kernels, shards(): pl.pallas_call(functools.partial(embed_kernel, n_edge), out_shape=(jax.Sh...  9.21 us
    pallas_call x1, Pallas kernels, shards(): pl.pallas_call(functools.partial(encode_kernel, n_edge, shard), out_shape...  3.95 us

profile of v5, /device:TPU:40, one launch (start us, length us, event | category | flops | bytes accessed | tf_op | source)
XLA Modules:
  0.0 71.1 jit_solution(6955465892178457310)
XLA Ops:
  1.3 9.2 %shard_map.248 = (s32[8,16,128]{2,1,0:T(8,128)S(1)}, bf16[8,4,2048]{2,1,0:T(4,128)(2,1)S(1)}, bf16[512,512]{1,0:T(8,128)(2,1)S(1)}, s32[8,1,256]{2,1,0:T(1,128)S...) custom-call(s32[1]{0:T(128)S(6)} %copy.27.count, s32[16,128]{1,0:T(8,128)} %bitcast.8, s32[16,128]{1,0:T(8,128)} %bitcast.9, ...), custom_call_target="tpu_custom_call" | custom-call | tf_op jit(solution)/shard_map/pallas_call | solution.py:809
  10.5 0.0 copy-start
  10.5 0.0 copy-start.1
  10.5 0.0 copy-start.2
  10.5 0.0 copy-start.3
  10.5 3.9 %shard_map.249.partial = bf16[128,512]{1,0:T(8,128)(2,1)S(1)} custom-call(s32[128,128]{1,0:T(8,128)S(1)} %bitcast.6, bf16[8,4,2048]{2,1,0:T(4,128)(2,1)S(1)} %get-tuple-element.11.features, bf16[512,512]{1,0:T(8,128)(2,1)S(1)} %get-tuple-element.12.projected, bf16[4,512]{1,0:T(4,128)(2,1)} %geometry.2), custom_call_target="tpu_custom_call" | custom-call | tf_op jit(solution)/shard_map/pallas_call | solution.py:849
  14.5 0.0 copy-done
  14.5 0.0 copy-done.1
  14.5 0.0 copy-done.2
  14.5 0.0 copy-done.3
  14.5 55.9 %shard_map.250 = (bf16[16,512]{1,0:T(8,128)(2,1)S(1)}, f32[16,512]{1,0:T(8,128)S(1)}) custom-call(bf16[128,512]{1,0:T(8,128)(2,1)S(1)} %shard_map.249.partial, bf16[3,16]{1,0:T(4,128)(2,1)S(1)} %copy-done.3, s32[8,1,256]{2,1,0:T(1,128)S(1)} %get-tuple-element.13.band_senders, s32[8,1,256]{2,1,0:T(1,128)S(1)} %get-tuple-element.14.band_receivers, ...), custom_call_target="tpu_custom_call" | custom-call | tf_op jit(solution)/shard_map/pallas_call | solution.py:881
  70.4 0.6 shard_map.251
Async XLA Ops:
  10.5 4.0 %copy-start = (bf16[16,512]{1,0:T(8,128)(2,1)S(1)}, bf16[16,512]{1,0:T(8,128)(2,1)}, u32[]{:S(2)}) copy-start(bf16[16,512]{1,0:T(8,128)(2,1)} %cotangent.1) | copy-start | bytes 49156
  10.5 4.0 %copy-start.1 = (bf16[3,512]{1,0:T(4,128)(2,1)S(1)}, bf16[3,512]{1,0:T(4,128)(2,1)}, u32[]{:S(2)}) copy-start(bf16[3,512]{1,0:T(4,128)(2,1)} %node_position.1) | copy-start | bytes 9220
  10.5 4.0 %copy-start.2 = (bf16[4,512]{1,0:T(4,128)(2,1)S(1)}, bf16[4,512]{1,0:T(4,128)(2,1)}, u32[]{:S(2)}) copy-start(bf16[4,512]{1,0:T(4,128)(2,1)} %geometry.3) | copy-start | bytes 12292
  10.5 4.0 %copy-start.3 = (bf16[3,16]{1,0:T(4,128)(2,1)S(1)}, bf16[3,16]{1,0:T(4,128)(2,1)}, u32[]{:S(2)}) copy-start(bf16[3,16]{1,0:T(4,128)(2,1)} %mesh_position.1) | copy-start | bytes 292

commit v6 on v5

--- a/solution.py
+++ b/solution.py
@@ -96,9 +96,6 @@
     senders,
     receivers,
     features,
-    mesh_senders,
-    mesh_receivers,
-    mesh_features,
     grid_input,
     first,
     second,
@@ -106,9 +103,6 @@
     packed_all,
     features_all,
     projected,
-    band_senders,
-    band_receivers,
-    band_features,
     senders_v,
     receivers_v,
     rows_v,
@@ -128,9 +122,6 @@
                 (senders, senders_v),
                 (receivers, receivers_v),
                 (features, features_all.at[me]),
-                (mesh_senders, band_senders.at[me]),
-                (mesh_receivers, band_receivers.at[me]),
-                (mesh_features, band_features.at[me]),
                 (grid_input, rows_v),
                 (first, first_v),
                 (second, second_v),
@@ -150,11 +141,10 @@
     near = receivers_v[...] - band * shard
     live = iota((blocks, BLOCK), 0) < count[0]
     packed_all[me] = jnp.where(live, low * shard + near, -1)
-    for load in loads[2:6]:
-        load.wait()
+    loads[2].wait()
     pl.semaphore_wait(pltpu.get_barrier_semaphore(), n_edge - 1)
 
-    tables = (packed_all, features_all, band_senders, band_receivers, band_features)
+    tables = (packed_all, features_all)
 
     def copy(k, owner, peer):
         return pltpu.make_async_remote_copy(
@@ -166,15 +156,14 @@
             device_id_type=MESH,
         )
 
-    for group in ((0, 1), (2, 3, 4)):
-        each_peer(n_edge, lambda own, peer: [copy(k, own, peer).start() for k in group])
-    loads[6].wait()
-    loads[7].wait()
+    each_peer(n_edge, lambda own, peer: [copy(k, own, peer).start() for k in range(len(tables))])
+    loads[3].wait()
+    loads[4].wait()
     hidden = tn(rows_v[...], first_v[...])
     hidden = (hidden * sigmoid(hidden)).astype(BF16)
-    loads[8].wait()
+    loads[5].wait()
     latent = layer_norm(nn(hidden, second_v[...])).astype(BF16)
-    loads[9].wait()
+    loads[6].wait()
     projected[...] = tt(inner_v[...], latent).astype(BF16)
 
     def arrive(own, peer):
@@ -335,9 +324,9 @@
     n_edge,
     partial,
     mesh_position,
-    band_senders,
-    band_receivers,
-    band_features,
+    mesh_senders,
+    mesh_receivers,
+    mesh_features,
     cotangent,
     node_position,
     geometry,
@@ -368,6 +357,9 @@
     coarse_own,
     coarse_land,
     coarse,
+    band_senders,
+    band_receivers,
+    band_features,
     send_pick,
     recv_pick,
     recv_drop,
@@ -403,7 +395,7 @@
     shard = own_rows * n_edge
     groups = n_mesh * COARSE // own_rows
     per_group = own_rows // COARSE
-    half = band_senders.shape[2]
+    half = mesh_senders.shape[1]
     edges = 2 * half
     far_rows = n_mesh * COARSE
     loads = [
@@ -497,6 +489,14 @@
     own_slice = pl.ds(pl.multiple_of(me * own_rows, own_rows), own_rows)
     start_all(0, rows_of(partial), enc_land)
     enc_land[me] = partial[own_slice, :]
+    tables = (
+        (3, mesh_senders, band_senders),
+        (4, mesh_receivers, band_receivers),
+        (5, mesh_features, band_features),
+    )
+    for phase, src, dst in tables:
+        start_all(phase, lambda peer: src, dst)
+        dst[me] = src[...]
 
     padded[...] = jnp.zeros_like(padded)
     padded[0:3, 0:own_rows] = mesh_position[...].astype(F32)
@@ -508,6 +508,52 @@
         )
 
     width = geometry.shape[1]
+    for load in loads:
+        load.wait()
+    enc_node[...] = nn(encoder_outer[...], node_first[...]).astype(BF16)
+
+    wait_all(0, rows_of(partial), enc_land)
+
+    @pl.when(core == 1)
+    def _():
+        pl.semaphore_wait(barrier, 2 * (n_mesh - 1))
+        pl.semaphore_signal(far_ready, inc=1, device_id={"edge": me ^ 1}, device_id_type=MESH)
+
+    enc_sum = jnp.sum(enc_land[...].astype(F32), axis=0)
+    hidden = nn(enc_sum.astype(BF16), enc_node[...]) + position_term
+    hidden = (hidden * sigmoid(hidden)).astype(BF16)
+    latent = layer_norm(nn(hidden, node_second[...])).astype(BF16)
+    coarse_own[...] = latent[0:COARSE, :]
+    latents[me] = latent
+
+    latent_rows = lambda peer: latents.at[me]
+
+    def far_copy(place, land):
+        return pltpu.make_async_remote_copy(
+            src_ref=coarse_own,
+            dst_ref=coarse_land.at[land],
+            send_sem=far_send.at[place],
+            recv_sem=far_recv.at[land],
+            device_id={"mesh": (band + step_of(place) + n_mesh) & (n_mesh - 1)},
+            device_id_type=MESH,
+        )
+
+    def far_start(k, carry):
+        place = n_mesh - k
+        far_copy(place, place_of(-step_of(place), n_mesh)).start()
+        return carry
+
+    @pl.when(core == 0)
+    def _():
+        pl.semaphore_wait(far_ready, 1)
+
+    lax.fori_loop(1, n_mesh, far_start, 0)
+    start_all(1, latent_rows, latents)
+    start_all(2, lambda peer: cotangent, cotangents)
+    cotangents[me] = cotangent[...]
+    coarse_land[0] = coarse_own[...]
+    for phase, src, dst in tables:
+        wait_all(phase, lambda peer: src, dst)
     padded_geometry = jnp.concatenate([geometry[...].astype(F32)] * 2, axis=0)
     padded_geometry = jnp.where(iota((8, width), 0) < 4, padded_geometry, 0.0).astype(BF16)
     small[...] = jnp.zeros_like(small)
@@ -554,49 +600,6 @@
         return carry
 
     lax.fori_loop(0, blocks, prepare, 0)
-    for load in loads:
-        load.wait()
-    enc_node[...] = nn(encoder_outer[...], node_first[...]).astype(BF16)
-
-    wait_all(0, rows_of(partial), enc_land)
-    enc_sum = jnp.sum(enc_land[...].astype(F32), axis=0)
-    hidden = nn(enc_sum.astype(BF16), enc_node[...]) + position_term
-    hidden = (hidden * sigmoid(hidden)).astype(BF16)
-    latent = layer_norm(nn(hidden, node_second[...])).astype(BF16)
-    coarse_own[...] = latent[0:COARSE, :]
-    latents[me] = latent
-
-    latent_rows = lambda peer: latents.at[me]
-    start_all(1, latent_rows, latents)
-    start_all(2, lambda peer: cotangent, cotangents)
-    cotangents[me] = cotangent[...]
-
-    def far_copy(place, land):
-        return pltpu.make_async_remote_copy(
-            src_ref=coarse_own,
-            dst_ref=coarse_land.at[land],
-            send_sem=far_send.at[place],
-            recv_sem=far_recv.at[land],
-            device_id={"mesh": (band + step_of(place) + n_mesh) & (n_mesh - 1)},
-            device_id_type=MESH,
-        )
-
-    def far_start(k, carry):
-        place = n_mesh - k
-        far_copy(place, place_of(-step_of(place), n_mesh)).start()
-        return carry
-
-    @pl.when(core == 1)
-    def _():
-        pl.semaphore_wait(barrier, 2 * (n_mesh - 1))
-        pl.semaphore_signal(far_ready, inc=1, device_id={"edge": me ^ 1}, device_id_type=MESH)
-
-    @pl.when(core == 0)
-    def _():
-        pl.semaphore_wait(far_ready, 1)
-
-    lax.fori_loop(1, n_mesh, far_start, 0)
-    coarse_land[0] = coarse_own[...]
 
     def relay(group, owner, peer):
         return pltpu.make_async_remote_copy(
@@ -633,8 +636,11 @@
         unsent.append(copy)
 
     def take_in(group):
-        each_chip(n_edge, lambda peer: forward(group, peer ^ 1).wait_recv())
-        relay(group, me ^ 1, me).wait_recv()
+        if group == groups - 1:
+            each_peer(n_edge, lambda own, peer: relay(group, peer, me).wait_recv())
+        else:
+            each_chip(n_edge, lambda peer: forward(group, peer ^ 1).wait_recv())
+            relay(group, me ^ 1, me).wait_recv()
         table = coarse[:, group].reshape(n_edge * own_rows, width)
         table = nn(table, edge_sender[...]).astype(BF16)
         return pl.ds(shard + group * n_edge * own_rows, n_edge * own_rows), table
@@ -674,15 +680,17 @@
                 far_copy(place, place).wait_recv()
         rows = [coarse_land[group * per_group + k].astype(F32) for k in range(per_group)]
         coarse[me, group] = jnp.concatenate(rows, axis=0).astype(BF16)
-        each_chip(n_edge, lambda peer: relay_start(group, peer))
-        relay_start(group, me ^ 1)
+        if group == groups - 1:
+            each_peer(n_edge, lambda own, peer: relay_start(group, peer))
+        else:
+            each_chip(n_edge, lambda peer: relay_start(group, peer))
+            relay_start(group, me ^ 1)
         if group > 0:
             pass_on(group - 1)
         if group > 1:
             add_in(group - 2)
     if groups > 1:
         add_in(groups - 2)
-    pass_on(groups - 1)
     columns, table = take_in(groups - 1)
     proc_sum = jnp.zeros((shard, width), F32)
     for block in range(blocks):
@@ -806,18 +814,15 @@
     shard = own_rows * n_edge
     edges = mesh_senders.shape[0]
     dma = pltpu.SemaphoreType.DMA
-    packed, features, projected, band_senders, band_receivers, band_features = pl.pallas_call(
+    packed, features, projected = pl.pallas_call(
         functools.partial(embed_kernel, n_edge),
         out_shape=(
             jax.ShapeDtypeStruct((n_edge, blocks, BLOCK), I32),
             jax.ShapeDtypeStruct((n_edge, 4, slots), BF16),
             jax.ShapeDtypeStruct((width, grid_rows), BF16),
-            jax.ShapeDtypeStruct((n_edge, 1, edges), I32),
-            jax.ShapeDtypeStruct((n_edge, 1, edges), I32),
-            jax.ShapeDtypeStruct((n_edge, 4, edges), BF16),
         ),
-        in_specs=[pl.BlockSpec(memory_space=pltpu.SMEM)] + [anywhere()] * 10,
-        out_specs=(vmem(),) * 6,
+        in_specs=[pl.BlockSpec(memory_space=pltpu.SMEM)] + [anywhere()] * 7,
+        out_specs=(vmem(),) * 3,
         scratch_shapes=[
             pltpu.VMEM((blocks, BLOCK), I32),
             pltpu.VMEM((blocks, BLOCK), I32),
@@ -825,9 +830,9 @@
             pltpu.VMEM((channels, width), BF16),
             pltpu.VMEM((width, width), BF16),
             pltpu.VMEM((width, width), BF16),
-            dma((10,)),
-            dma((5, n_edge)),
-            dma((5, n_edge)),
+            dma((7,)),
+            dma((2, n_edge)),
+            dma((2, n_edge)),
         ],
         compiler_params=pltpu.CompilerParams(
             collective_id=0, has_side_effects=True, vmem_limit_bytes=12 << 20
@@ -837,9 +842,6 @@
         hbm(encoder_senders.reshape(blocks, BLOCK)),
         hbm(encoder_receivers.reshape(blocks, BLOCK)),
         hbm(encoder_features),
-        hbm(mesh_senders.reshape(1, edges)),
-        hbm(mesh_receivers.reshape(1, edges)),
-        hbm(mesh_features),
         hbm(grid_input.T),
         hbm(grid_first),
         hbm(grid_second),
@@ -895,6 +897,9 @@
             pltpu.VMEM((COARSE, width), BF16),
             pltpu.VMEM((n_mesh, COARSE, width), BF16),
             pltpu.VMEM((n_edge, groups, own_rows, width), BF16),
+            pltpu.VMEM((n_edge, 1, edges), I32),
+            pltpu.VMEM((n_edge, 1, edges), I32),
+            pltpu.VMEM((n_edge, 4, edges), BF16),
             pltpu.VMEM((n_edge * edges, table_rows), BF16),
             pltpu.VMEM((n_edge * edges, shard), BF16),
             pltpu.VMEM((shard, n_edge * edges), BF16),
@@ -912,8 +917,8 @@
             pltpu.VMEM((width, width), BF16),
             pltpu.VMEM((width, width), BF16),
             dma((9,)),
-            dma((3, n_edge)),
-            dma((3, n_edge)),
+            dma((6, n_edge)),
+            dma((6, n_edge)),
             dma((n_mesh,)),
             dma((n_mesh,)),
             dma((groups, n_edge)),
@@ -930,9 +935,9 @@
     )(
         partial,
         mesh_position,
-        band_senders,
-        band_receivers,
-        band_features,
+        mesh_senders.reshape(1, edges),
+        mesh_receivers.reshape(1, edges),
+        mesh_features,
         cotangent,
         node_position,
         edge_geometry,

time: 72.3 us -> 71.8 us (level); the launches traced: 71.1 us -> 71.7 us
    pallas_call x1, Pallas kernels: 55.9 us -> 58 us  [shards(): pl.pallas_call(functools.partial(process_kernel, n_mesh, n_edge), out_sha...]
    pallas_call x1, Pallas kernels: 9.21 us -> 7.63 us  [shards(): pl.pallas_call(functools.partial(embed_kernel, n_edge), out_shape=(jax.Sh...]
where the time goes in v6:
time: 71.8 us; the launch traced here: 71.7 us
  Pallas kernels  70.2 us (98%)
  between operations  1.41 us (2%)
    pallas_call x1, Pallas kernels, shards(): pl.pallas_call(functools.partial(process_kernel, n_mesh, n_edge), out_sha...  58 us
    pallas_call x1, Pallas kernels, shards(): pl.pallas_call(functools.partial(embed_kernel, n_edge), out_shape=(jax.Sh...  7.63 us
    pallas_call x1, Pallas kernels, shards(): pl.pallas_call(functools.partial(encode_kernel, n_edge, shard), out_shape...  3.91 us

profile of v6, /device:TPU:40, one launch (start us, length us, event | category | flops | bytes accessed | tf_op | source)
XLA Modules:
  0.0 71.7 jit_solution(4006021898019659136)
XLA Ops:
  1.3 7.6 %shard_map.248 = (s32[8,16,128]{2,1,0:T(8,128)S(1)}, bf16[8,4,2048]{2,1,0:T(4,128)(2,1)S(1)}, bf16[512,512]{1,0:T(8,128)(2,1)S(1)}) custom-call(s32[1]{0:T(128)S(6)} %copy.27.count, s32[16,128]{1,0:T(8,128)} %bitcast.10, s32[16,128]{1,0:T(8,128)} %bitcast.11, bf16[4,2048]{1,0:T(4,128)(2,1)} %features.1, bf16[474,512]{1,0:T(8,128)(2,1)} %bitcast.9, ...), custom_call_target="tpu_custom_call" | custom-call | tf_op jit(solution)/shard_map/pallas_call | solution.py:817
  8.9 0.0 copy-start
  8.9 0.0 copy-start.1
  8.9 0.0 copy-start.2
  9.0 0.0 copy-start.3
  9.0 0.0 copy-start.4
  9.0 0.0 copy-start.5
  9.0 0.0 copy-start.6
  9.0 3.9 %shard_map.249.partial = bf16[128,512]{1,0:T(8,128)(2,1)S(1)} custom-call(s32[128,128]{1,0:T(8,128)S(1)} %bitcast.6, bf16[8,4,2048]{2,1,0:T(4,128)(2,1)S(1)} %get-tuple-element.8.features, bf16[512,512]{1,0:T(8,128)(2,1)S(1)} %get-tuple-element.9.projected, bf16[4,512]{1,0:T(4,128)(2,1)} %geometry.2), custom_call_target="tpu_custom_call" | custom-call | tf_op jit(solution)/shard_map/pallas_call | solution.py:851
  12.9 0.0 copy-done
  12.9 0.0 copy-done.1
  12.9 0.0 copy-done.2
  12.9 0.0 copy-done.3
  13.0 0.0 copy-done.4
  13.0 0.0 copy-done.5
  13.0 0.0 copy-done.6
  13.0 58.0 %shard_map.250 = (bf16[16,512]{1,0:T(8,128)(2,1)S(1)}, f32[16,512]{1,0:T(8,128)S(1)}) custom-call(bf16[128,512]{1,0:T(8,128)(2,1)S(1)} %shard_map.249.partial, bf16[3,16]{1,0:T(4,128)(2,1)S(1)} %copy-done.4, s32[1,256]{1,0:T(1,128)S(1)} %bitcast.7, s32[1,256]{1,0:T(1,128)S(1)} %bitcast.8, bf16[4,256]{1,0:T(4,128)(2,1)S(1)} %copy-done.3, ...), custom_call_target="tpu_custom_call" | custom-call | tf_op jit(solution)/shard_map/pallas_call | solution.py:883
  71.0 0.6 shard_map.251
Async XLA Ops:
  8.9 4.0 %copy-start = (bf16[16,512]{1,0:T(8,128)(2,1)S(1)}, bf16[16,512]{1,0:T(8,128)(2,1)}, u32[]{:S(2)}) copy-start(bf16[16,512]{1,0:T(8,128)(2,1)} %cotangent.1) | copy-start | bytes 49156
  8.9 4.0 %copy-start.1 = (bf16[3,512]{1,0:T(4,128)(2,1)S(1)}, bf16[3,512]{1,0:T(4,128)(2,1)}, u32[]{:S(2)}) copy-start(bf16[3,512]{1,0:T(4,128)(2,1)} %node_position.1) | copy-start | bytes 9220
  8.9 4.0 %copy-start.2 = (bf16[4,512]{1,0:T(4,128)(2,1)S(1)}, bf16[4,512]{1,0:T(4,128)(2,1)}, u32[]{:S(2)}) copy-start(bf16[4,512]{1,0:T(4,128)(2,1)} %geometry.3) | copy-start | bytes 12292
  9.0 4.0 %copy-start.3 = (bf16[4,256]{1,0:T(4,128)(2,1)S(1)}, bf16[4,256]{1,0:T(4,128)(2,1)}, u32[]{:S(2)}) copy-start(bf16[4,256]{1,0:T(4,128)(2,1)} %mesh_features.1) | copy-start | bytes 6148
  9.0 4.0 %copy-start.4 = (bf16[3,16]{1,0:T(4,128)(2,1)S(1)}, bf16[3,16]{1,0:T(4,128)(2,1)}, u32[]{:S(2)}) copy-start(bf16[3,16]{1,0:T(4,128)(2,1)} %mesh_position.1) | copy-start | bytes 292
  9.0 4.0 %copy-start.5 = (s32[256]{0:T(256)S(1)}, s32[256]{0:T(256)}, u32[]{:S(2)}) copy-start(s32[256]{0:T(256)} %param.31) | copy-start | bytes 3076
  9.0 4.0 %copy-start.6 = (s32[256]{0:T(256)S(1)}, s32[256]{0:T(256)}, u32[]{:S(2)}) copy-start(s32[256]{0:T(256)} %param.32) | copy-start | bytes 3076

commit v7 on v5

--- a/solution.py
+++ b/solution.py
@@ -106,11 +106,10 @@
     packed_all,
     features_all,
     projected,
-    band_senders,
-    band_receivers,
-    band_features,
     senders_v,
     receivers_v,
+    near_senders_v,
+    near_receivers_v,
     rows_v,
     first_v,
     second_v,
@@ -121,16 +120,18 @@
 ):
     me = lax.axis_index("edge")
     band = lax.axis_index("mesh")
+    slots = features.shape[1]
+    mesh_slots = mesh_features.shape[1]
     loads = [
         pltpu.make_async_copy(src, dst, load_sem.at[k])
         for k, (src, dst) in enumerate(
             [
                 (senders, senders_v),
                 (receivers, receivers_v),
-                (features, features_all.at[me]),
-                (mesh_senders, band_senders.at[me]),
-                (mesh_receivers, band_receivers.at[me]),
-                (mesh_features, band_features.at[me]),
+                (mesh_senders, near_senders_v),
+                (mesh_receivers, near_receivers_v),
+                (features, features_all.at[me, :, pl.ds(0, slots)]),
+                (mesh_features, features_all.at[me, :, pl.ds(slots, mesh_slots)]),
                 (grid_input, rows_v),
                 (first, first_v),
                 (second, second_v),
@@ -144,17 +145,20 @@
     blocks = senders.shape[0]
     rows = grid_input.shape[1]
     shard = packed_shard(n_edge)
-    loads[0].wait()
-    loads[1].wait()
+    for load in loads[0:4]:
+        load.wait()
     low = senders_v[...] - band * (rows * n_edge)
     near = receivers_v[...] - band * shard
     live = iota((blocks, BLOCK), 0) < count[0]
-    packed_all[me] = jnp.where(live, low * shard + near, -1)
-    for load in loads[2:6]:
+    packed_all[me, 0:blocks, :] = jnp.where(live, low * shard + near, -1)
+    code = near_senders_v[...] * shard + near_receivers_v[...] - band * shard
+    code = jnp.concatenate([code, jnp.zeros((8 - code.shape[0], BLOCK), I32)], axis=0)
+    packed_all[me, blocks : blocks + 8, :] = code
+    for load in loads[4:6]:
         load.wait()
     pl.semaphore_wait(pltpu.get_barrier_semaphore(), n_edge - 1)
 
-    tables = (packed_all, features_all, band_senders, band_receivers, band_features)
+    tables = (packed_all, features_all)
 
     def copy(k, owner, peer):
         return pltpu.make_async_remote_copy(
@@ -166,8 +170,7 @@
             device_id_type=MESH,
         )
 
-    for group in ((0, 1), (2, 3, 4)):
-        each_peer(n_edge, lambda own, peer: [copy(k, own, peer).start() for k in group])
+    each_peer(n_edge, lambda own, peer: [copy(k, own, peer).start() for k in range(len(tables))])
     loads[6].wait()
     loads[7].wait()
     hidden = tn(rows_v[...], first_v[...])
@@ -201,6 +204,7 @@
     projected,
     geometry,
     partial,
+    encoded,
     position,
     bounds_v,
     bounds,
@@ -214,13 +218,14 @@
     me = lax.axis_index("edge")
     load = pltpu.make_async_copy(geometry, geometry_w, geometry_sem)
     load.start()
-    blocks = packed.shape[0]
-    per_device = blocks // n_edge
+    per_device = packed.shape[1] - 8
+    blocks = per_device * n_edge
     grid_rows = projected.shape[1]
     width = projected.shape[0]
     shift = bits(shard)
     row_bits = bits(grid_rows)
-    index = packed[...]
+    index = jnp.concatenate([packed[k, 0:per_device, :] for k in range(n_edge)], axis=0)
+    encoded[...] = index
     own = (index >> (shift + row_bits)) == me
     own_b = one_hot(own)
     upper = one_hot(iota((BLOCK, BLOCK), 0) < iota((BLOCK, BLOCK), 1))
@@ -245,7 +250,7 @@
     per_chunk = per_device // CHUNK_ROWS
 
     def chunk_of(c, device, lane, row):
-        code = packed[pl.ds(row, CHUNK_ROWS), :]
+        code = encoded[pl.ds(row, CHUNK_ROWS), :]
         where = position[pl.ds(row, CHUNK_ROWS), :]
         code_row = jnp.concatenate([code[k : k + 1, :] for k in range(CHUNK_ROWS)], axis=1)
         where_row = jnp.concatenate([where[k : k + 1, :] for k in range(CHUNK_ROWS)], axis=1)
@@ -333,11 +338,11 @@
 def process_kernel(
     n_mesh,
     n_edge,
+    mesh_slots,
     partial,
     mesh_position,
-    band_senders,
-    band_receivers,
-    band_features,
+    packed,
+    features,
     cotangent,
     node_position,
     geometry,
@@ -403,7 +408,10 @@
     shard = own_rows * n_edge
     groups = n_mesh * COARSE // own_rows
     per_group = own_rows // COARSE
-    half = band_senders.shape[2]
+    mesh_blocks = mesh_slots // BLOCK
+    half = mesh_slots
+    slots = features.shape[2] - half
+    first_row = packed.shape[1] - 8
     edges = 2 * half
     far_rows = n_mesh * COARSE
     loads = [
@@ -497,6 +505,8 @@
     own_slice = pl.ds(pl.multiple_of(me * own_rows, own_rows), own_rows)
     start_all(0, rows_of(partial), enc_land)
     enc_land[me] = partial[own_slice, :]
+    start_all(2, lambda peer: cotangent, cotangents)
+    cotangents[me] = cotangent[...]
 
     padded[...] = jnp.zeros_like(padded)
     padded[0:3, 0:own_rows] = mesh_position[...].astype(F32)
@@ -520,8 +530,12 @@
     def prepare(block, carry):
         span = block_rows(block)
         first, second = 2 * block, 2 * block + 1
-        sender = jnp.concatenate([band_senders[first], band_senders[second]], axis=1)
-        receiver = jnp.concatenate([band_receivers[first], band_receivers[second]], axis=1)
+        codes = [packed[device, first_row : first_row + 8, :] for device in (first, second)]
+        code = jnp.concatenate(
+            [rows[k : k + 1, :] for rows in codes for k in range(mesh_blocks)], axis=1
+        )
+        sender = code >> bits(shard)
+        receiver = code & (shard - 1)
         owner_band = sender >> bits(shard)
         near = owner_band == band
         owner_edge = (sender >> bits(own_rows)) & (n_edge - 1)
@@ -530,7 +544,6 @@
         far_slot = ((far_place >> bits(per_group)) * n_edge + owner_edge) * own_rows
         far_slot = far_slot + (far_place & (per_group - 1)) * COARSE + coarse_row
         local = sender - band * shard
-        receiver = receiver - band * shard
         pick = jnp.where(near, local, shard + far_slot)
         mine = owner_edge == me
         drop_far = jnp.where(mine & (owner_band != band), far_place * COARSE + coarse_row, -1)
@@ -548,8 +561,8 @@
             send_pick[span, k * 128 : (k + 1) * 128] = one_hot(lanes + k * 128 == pick_columns)
         for k in range(shard // 128):
             recv_pick[span, k * 128 : (k + 1) * 128] = one_hot(lanes + k * 128 == recv_columns)
-        small[0:4, 0:half] = band_features[first].astype(F32)
-        small[0:4, half:edges] = band_features[second].astype(F32)
+        small[0:4, 0:half] = features[first, :, slots:].astype(F32)
+        small[0:4, half:edges] = features[second, :, slots:].astype(F32)
         edge_term[span, :] = tn(small[...].astype(BF16), padded_geometry)
         return carry
 
@@ -568,8 +581,6 @@
 
     latent_rows = lambda peer: latents.at[me]
     start_all(1, latent_rows, latents)
-    start_all(2, lambda peer: cotangent, cotangents)
-    cotangents[me] = cotangent[...]
 
     def far_copy(place, land):
         return pltpu.make_async_remote_copy(
@@ -633,8 +644,11 @@
         unsent.append(copy)
 
     def take_in(group):
-        each_chip(n_edge, lambda peer: forward(group, peer ^ 1).wait_recv())
-        relay(group, me ^ 1, me).wait_recv()
+        if group == groups - 1:
+            each_peer(n_edge, lambda own, peer: relay(group, peer, me).wait_recv())
+        else:
+            each_chip(n_edge, lambda peer: forward(group, peer ^ 1).wait_recv())
+            relay(group, me ^ 1, me).wait_recv()
         table = coarse[:, group].reshape(n_edge * own_rows, width)
         table = nn(table, edge_sender[...]).astype(BF16)
         return pl.ds(shard + group * n_edge * own_rows, n_edge * own_rows), table
@@ -674,15 +688,17 @@
                 far_copy(place, place).wait_recv()
         rows = [coarse_land[group * per_group + k].astype(F32) for k in range(per_group)]
         coarse[me, group] = jnp.concatenate(rows, axis=0).astype(BF16)
-        each_chip(n_edge, lambda peer: relay_start(group, peer))
-        relay_start(group, me ^ 1)
+        if group == groups - 1:
+            each_peer(n_edge, lambda own, peer: relay_start(group, peer))
+        else:
+            each_chip(n_edge, lambda peer: relay_start(group, peer))
+            relay_start(group, me ^ 1)
         if group > 0:
             pass_on(group - 1)
         if group > 1:
             add_in(group - 2)
     if groups > 1:
         add_in(groups - 2)
-    pass_on(groups - 1)
     columns, table = take_in(groups - 1)
     proc_sum = jnp.zeros((shard, width), F32)
     for block in range(blocks):
@@ -806,28 +822,27 @@
     shard = own_rows * n_edge
     edges = mesh_senders.shape[0]
     dma = pltpu.SemaphoreType.DMA
-    packed, features, projected, band_senders, band_receivers, band_features = pl.pallas_call(
+    packed, features, projected = pl.pallas_call(
         functools.partial(embed_kernel, n_edge),
         out_shape=(
-            jax.ShapeDtypeStruct((n_edge, blocks, BLOCK), I32),
-            jax.ShapeDtypeStruct((n_edge, 4, slots), BF16),
+            jax.ShapeDtypeStruct((n_edge, blocks + 8, BLOCK), I32),
+            jax.ShapeDtypeStruct((n_edge, 4, slots + edges), BF16),
             jax.ShapeDtypeStruct((width, grid_rows), BF16),
-            jax.ShapeDtypeStruct((n_edge, 1, edges), I32),
-            jax.ShapeDtypeStruct((n_edge, 1, edges), I32),
-            jax.ShapeDtypeStruct((n_edge, 4, edges), BF16),
         ),
         in_specs=[pl.BlockSpec(memory_space=pltpu.SMEM)] + [anywhere()] * 10,
-        out_specs=(vmem(),) * 6,
+        out_specs=(vmem(),) * 3,
         scratch_shapes=[
             pltpu.VMEM((blocks, BLOCK), I32),
             pltpu.VMEM((blocks, BLOCK), I32),
+            pltpu.VMEM((edges // BLOCK, BLOCK), I32),
+            pltpu.VMEM((edges // BLOCK, BLOCK), I32),
             pltpu.VMEM((channels, grid_rows), BF16),
             pltpu.VMEM((channels, width), BF16),
             pltpu.VMEM((width, width), BF16),
             pltpu.VMEM((width, width), BF16),
             dma((10,)),
-            dma((5, n_edge)),
-            dma((5, n_edge)),
+            dma((2, n_edge)),
+            dma((2, n_edge)),
         ],
         compiler_params=pltpu.CompilerParams(
             collective_id=0, has_side_effects=True, vmem_limit_bytes=12 << 20
@@ -837,8 +852,8 @@
         hbm(encoder_senders.reshape(blocks, BLOCK)),
         hbm(encoder_receivers.reshape(blocks, BLOCK)),
         hbm(encoder_features),
-        hbm(mesh_senders.reshape(1, edges)),
-        hbm(mesh_receivers.reshape(1, edges)),
+        hbm(mesh_senders.reshape(edges // BLOCK, BLOCK)),
+        hbm(mesh_receivers.reshape(edges // BLOCK, BLOCK)),
         hbm(mesh_features),
         hbm(grid_input.T),
         hbm(grid_first),
@@ -853,6 +868,7 @@
         out_specs=vmem(),
         scratch_shapes=[
             pltpu.VMEM((all_blocks, BLOCK), I32),
+            pltpu.VMEM((all_blocks, BLOCK), I32),
             pltpu.VMEM((8, all_blocks), I32),
             pltpu.SMEM((8, all_blocks), I32),
             pltpu.VMEM((8, n_edge * slots + STEP), F32),
@@ -863,7 +879,7 @@
             dma(()),
         ],
         compiler_params=pltpu.CompilerParams(vmem_limit_bytes=16 << 20),
-    )(packed.reshape(all_blocks, BLOCK), features, projected, hbm(encoder_geometry))
+    )(packed, features, projected, hbm(encoder_geometry))
     far_rows = n_mesh * COARSE
     groups = far_rows // own_rows
     table_rows = shard + n_edge * far_rows
@@ -879,12 +895,12 @@
         update_outer,
     ]
     output, gradient = pl.pallas_call(
-        functools.partial(process_kernel, n_mesh, n_edge),
+        functools.partial(process_kernel, n_mesh, n_edge, edges),
         out_shape=(
             jax.ShapeDtypeStruct((own_rows, width), BF16),
             jax.ShapeDtypeStruct((own_rows, width), F32),
         ),
-        in_specs=[vmem()] * 8 + [anywhere()] * 9,
+        in_specs=[vmem()] * 7 + [anywhere()] * 9,
         out_specs=(vmem(), vmem()),
         scratch_shapes=[pltpu.VMEM((width, width), BF16) for _ in weights]
         + [
@@ -930,9 +946,8 @@
     )(
         partial,
         mesh_position,
-        band_senders,
-        band_receivers,
-        band_features,
+        packed,
+        features,
         cotangent,
         node_position,
         edge_geometry,

time: 72.3 us -> 70.2 us (0.971)
  Pallas kernels: 69.7 us -> 68 us
    pallas_call x1, Pallas kernels: 9.21 us -> 8.27 us  [shards(): pl.pallas_call(functools.partial(embed_kernel, n_edge), out_shape=(jax.Sh...]
where the time goes in v7:
time: 70.2 us; the launch traced here: 69.4 us
  Pallas kernels  68 us (97%)
  between operations  1.37 us (2%)
    pallas_call x1, Pallas kernels, shards(): pl.pallas_call(functools.partial(process_kernel, n_mesh, n_edge, edges),...  55.3 us
    pallas_call x1, Pallas kernels, shards(): pl.pallas_call(functools.partial(embed_kernel, n_edge), out_shape=(jax.Sh...  8.27 us
    pallas_call x1, Pallas kernels, shards(): pl.pallas_call(functools.partial(encode_kernel, n_edge, shard), out_shape...  3.84 us

profile of v7, /device:TPU:40, one launch (start us, length us, event | category | flops | bytes accessed | tf_op | source)
XLA Modules:
  0.0 69.4 jit_solution(3237212831792970886)
XLA Ops:
  1.3 8.3 %shard_map.248 = (s32[8,24,128]{2,1,0:T(8,128)S(1)}, bf16[8,4,2304]{2,1,0:T(4,128)(2,1)S(1)}, bf16[512,512]{1,0:T(8,128)(2,1)S(1)}) custom-call(s32[1]{0:T(128)S(6)} %copy.27.count, s32[16,128]{1,0:T(8,128)} %bitcast.6, s32[16,128]{1,0:T(8,128)} %bitcast.7, bf16[4,2048]{1,0:T(4,128)(2,1)} %features.1, s32[2,128]{1,0:T(2,128)} %bitcast.8, s32[2,128]{1,0:T(2,128)} %bitcast.9, ...), custom_call_target="tpu_custom_call" | custom-call | tf_op jit(solution)/shard_map/pallas_call | solution.py:825
  9.6 0.0 copy-start
  9.6 0.0 copy-start.1
  9.6 0.0 copy-start.2
  9.6 0.0 copy-start.3
  9.6 3.8 %shard_map.249.partial = bf16[128,512]{1,0:T(8,128)(2,1)S(1)} custom-call(s32[8,24,128]{2,1,0:T(8,128)S(1)} %get-tuple-element.7.packed, bf16[8,4,2304]{2,1,0:T(4,128)(2,1)S(1)} %get-tuple-element.8.features, bf16[512,512]{1,0:T(8,128)(2,1)S(1)} %get-tuple-element.9.projected, bf16[4,512]{1,0:T(4,128)(2,1)} %geometry.2), custom_call_target="tpu_custom_call" | custom-call | tf_op jit(solution)/shard_map/pallas_call | solution.py:864
  13.4 0.0 copy-done
  13.5 0.0 copy-done.1
  13.5 0.0 copy-done.2
  13.5 0.0 copy-done.3
  13.5 55.3 %shard_map.250 = (bf16[16,512]{1,0:T(8,128)(2,1)S(1)}, f32[16,512]{1,0:T(8,128)S(1)}) custom-call(bf16[128,512]{1,0:T(8,128)(2,1)S(1)} %shard_map.249.partial, bf16[3,16]{1,0:T(4,128)(2,1)S(1)} %copy-done.3, s32[8,24,128]{2,1,0:T(8,128)S(1)} %get-tuple-element.7.packed, bf16[8,4,2304]{2,1,0:T(4,128)(2,1)S(1)} %get-tuple-element.8.features, ...), custom_call_target="tpu_custom_call" | custom-call | tf_op jit(solution)/shard_map/pallas_call | solution.py:897
  68.8 0.6 shard_map.251
Async XLA Ops:
  9.6 3.9 %copy-start = (bf16[16,512]{1,0:T(8,128)(2,1)S(1)}, bf16[16,512]{1,0:T(8,128)(2,1)}, u32[]{:S(2)}) copy-start(bf16[16,512]{1,0:T(8,128)(2,1)} %cotangent.1) | copy-start | bytes 49156
  9.6 3.9 %copy-start.1 = (bf16[3,512]{1,0:T(4,128)(2,1)S(1)}, bf16[3,512]{1,0:T(4,128)(2,1)}, u32[]{:S(2)}) copy-start(bf16[3,512]{1,0:T(4,128)(2,1)} %node_position.1) | copy-start | bytes 9220
  9.6 3.9 %copy-start.2 = (bf16[4,512]{1,0:T(4,128)(2,1)S(1)}, bf16[4,512]{1,0:T(4,128)(2,1)}, u32[]{:S(2)}) copy-start(bf16[4,512]{1,0:T(4,128)(2,1)} %geometry.3) | copy-start | bytes 12292
  9.6 3.9 %copy-start.3 = (bf16[3,16]{1,0:T(4,128)(2,1)S(1)}, bf16[3,16]{1,0:T(4,128)(2,1)}, u32[]{:S(2)}) copy-start(bf16[3,16]{1,0:T(4,128)(2,1)} %mesh_position.1) | copy-start | bytes 292
